TPU v7x, 32 devices: a whole 2x2x4 slice. The times are simulated.
32 devices in a mesh: comp: 8 (over z, y), band: 4 (over x, core).
Axes of the slice: x: 2, y: 2, z: 4, core: 2. Of those that a mesh axis runs over, the one named last changes fastest.
Arguments:
- spectrum: float32 [1152, 32, 4096], P('comp', 'band'), may hold values from 0.1 to 1
- currents: float32 [2, 32, 4096], P(None, 'band', 'comp'), may hold values from -4 to 4
- group_courant: float32 [32], replicated, may hold values from 0.1 to 0.35
- refraction: float32 [8, 32], replicated, may hold values from -0.25 to 0.25
- interp: float32 [1152, 1152], replicated, may hold values from -0.1875 to 0.1875
- sea_mask: int32 [32, 4096], replicated, may hold values 0 or 1
- depth_class: int32 [32, 4096], replicated, may hold values from 0 to 7
- owner_map: int32 [8], replicated, may hold values from 0 to 7, each once
Outputs:
- spectrum_out: float32 [1152, 32, 4096], P('comp', 'band')
- ocean_out: float32 [2, 32, 4096], P(None, 'band', 'comp')
Inputs may be any that keep to these rules, and one draw needn't show every extreme that they name: `owner_map`: each of 0 to 7 once.
All inputs are finite; a program needn't handle non-finite values.
Results may differ from a plain program's by a relative error of at most 0.000098.
Values sent between devices are 32-bit elements; how exact they have to be, the bound alone decides.
No kernel may reach another device: no remote copies, remote signals or barrier semaphores. Data moves between devices by JAX's collectives and lax.ppermute only.
A program may use at most 192 MiB of HBM per device.

v0:
```python
import math

import jax
import jax.numpy as jnp
from jax import lax
from jax.sharding import PartitionSpec as P

DIRS = 36
FREQ = 32
SUBSTEPS = 4


CURRENT_COURANT = 0.025
SOURCE_STEP = 0.5
STOKES_SCALE = 0.2
OCEAN_STEP = 0.5
VISCOSITY = 0.2
DRAG = 0.1
HIGHEST = lax.Precision.HIGHEST


def swapped(block, axis, apart):
    count = lax.axis_size(axis)
    route = []
    for low in range(count):
        high = low | 1 << apart
        if high != low and high < count:
            route += [(low, high), (high, low)]
    return lax.ppermute(block, axis, route)


def padded_2(value, sides, width):
    for axis, dim in sides:
        count, length = (lax.axis_size(axis), value.shape[dim])
        up = [(i, (i + 1) % count) for i in range(count - 1)]
        down = [(j, i) for i, j in up]
        last = lax.slice_in_dim(value, length - width, length, axis=dim)
        first = lax.slice_in_dim(value, 0, width, axis=dim)
        before = lax.ppermute(last, axis, up)
        after = lax.ppermute(first, axis, down)
        value = jnp.concatenate([before, value, after], axis=dim)
    return value


def reorder_tiles(values_in, tile_order, tile_count):
    lead_dim, row_count, col_count = values_in.shape
    pieces = values_in.reshape(lead_dim, row_count, tile_count, col_count // tile_count)
    return jnp.take(pieces, tile_order, axis=2).reshape(lead_dim, row_count, col_count)


def upwind(centre_val, behind, ahead_val, speeds):
    return jnp.maximum(speeds, 0.0) * (centre_val - behind) + jnp.minimum(speeds, 0.0) * (
        ahead_val - centre_val
    )


def direction_pair(centre):
    dir_count, row_count, col_count = centre.shape
    if dir_count % DIRS == 0:
        circles = centre.reshape(dir_count // DIRS, DIRS, row_count, col_count)
        before_dir = jnp.roll(circles, 1, axis=1).reshape(centre.shape)
        after_dir = jnp.roll(circles, -1, axis=1).reshape(centre.shape)
    else:
        edge_dirs = jnp.stack([centre[0], centre[dir_count - 1]])
        partner = swapped(edge_dirs, "comp", 0)
        before_dir = jnp.concatenate([partner[1:2], centre[: dir_count - 1]], axis=0)
        after_dir = jnp.concatenate([centre[1:], partner[0:1]], axis=0)
    return (before_dir, after_dir)


def advance(padded, lon_speed, lat_speed, dir_speed, ocean_rows):
    centre = padded[:, 1:-1]
    south_rows = padded[:, :-2]
    north_rows = padded[:, 2:]
    west_cols = jnp.roll(centre, 1, axis=2)
    east_cols = jnp.roll(centre, -1, axis=2)
    before_dir, after_dir = direction_pair(centre)
    change = (
        upwind(centre, west_cols, east_cols, lon_speed)
        + upwind(centre, south_rows, north_rows, lat_speed)
        + upwind(centre, before_dir, after_dir, dir_speed)
    )
    return ocean_rows[None] * (centre - change)


def coefficients(current_rows, class_rows, speeds, cosine, sines, columns):
    lon_speed = (
        speeds[:, None, None] * cosine[:, None, None] + CURRENT_COURANT * current_rows[0][None]
    )
    lat_speed = (
        speeds[:, None, None] * sines[:, None, None] + CURRENT_COURANT * current_rows[1][None]
    )
    turning = jnp.zeros((speeds.shape[0],) + class_rows.shape, jnp.float32)
    for level in range(columns.shape[0]):
        turning = (
            turning
            + (class_rows == level).astype(jnp.float32)[None] * columns[level][:, None, None]
        )
    return (lon_speed, lat_speed, turning * cosine[:, None, None])


def component_tables(component, group_courant, refraction):
    frequency = component // DIRS
    direction = component % DIRS
    angles = direction.astype(jnp.float32) * (2.0 * math.pi / DIRS)
    return (
        jnp.take(group_courant, frequency),
        jnp.cos(angles),
        jnp.sin(angles),
        jnp.take(refraction, frequency, axis=1),
    )


def stokes_weights(comp_total):
    component = jnp.arange(comp_total, dtype=jnp.int32)
    frequency = component // DIRS
    direction = component % DIRS
    angles = direction.astype(jnp.float32) * (2.0 * math.pi / DIRS)
    scales = STOKES_SCALE * (frequency + 1).astype(jnp.float32) / FREQ
    return jnp.stack([scales * jnp.cos(angles), scales * jnp.sin(angles)])


def source_local(points, interp, weights):
    comp_total, row_count, col_count = points.shape
    flat_spec = points.reshape(comp_total, row_count * col_count)
    forward = jnp.dot(interp, flat_spec, precision=HIGHEST, preferred_element_type=jnp.float32)
    backward = lax.dot_general(
        interp,
        flat_spec,
        (((0,), (0,)), ((), ())),
        precision=HIGHEST,
        preferred_element_type=jnp.float32,
    )
    updated = flat_spec + SOURCE_STEP * (
        forward * backward - 0.5 * flat_spec * (forward + backward)
    )
    drift_rows = jnp.dot(weights, updated, precision=HIGHEST, preferred_element_type=jnp.float32)
    return (
        updated.reshape(comp_total, row_count, col_count),
        drift_rows.reshape(2, row_count, col_count),
    )


def velocity_rows(current_real):
    return padded_2(current_real, (("band", 1),), 1)


def ocean_update(current_rows, ocean_rows, tile_index, tile_width, stokes, coriolis):
    wrapped = jnp.concatenate(
        [current_rows[:, :, -1:], current_rows, current_rows[:, :, :1]], axis=2
    )
    ocean_wrapped = jnp.concatenate([ocean_rows[:, -1:], ocean_rows, ocean_rows[:, :1]], axis=1)
    tile_start = tile_index * tile_width
    cur_tile = lax.dynamic_slice_in_dim(wrapped, tile_start, tile_width + 2, 2)
    ocean_tile = lax.dynamic_slice_in_dim(ocean_wrapped, tile_start, tile_width + 2, 1)
    masked_cur = cur_tile * ocean_tile[None]
    centre = masked_cur[:, 1:-1, 1:-1]
    laplace = (
        masked_cur[:, 1:-1, :-2]
        + masked_cur[:, 1:-1, 2:]
        + masked_cur[:, :-2, 1:-1]
        + masked_cur[:, 2:, 1:-1]
        - 4.0 * centre
    )
    sea_tile = ocean_tile[1:-1, 1:-1]
    east_new = sea_tile * (
        centre[0]
        + OCEAN_STEP
        * (coriolis * (centre[1] + stokes[1]) + VISCOSITY * laplace[0] - DRAG * centre[0])
    )
    north_new = sea_tile * (
        centre[1]
        + OCEAN_STEP
        * (-coriolis * (centre[0] + stokes[0]) + VISCOSITY * laplace[1] - DRAG * centre[1])
    )
    return jnp.stack([east_new, north_new])


def local(spectrum, currents, group_courant, refraction, interp, sea_mask, depth_class, owner_map):
    per_device, rows_dev, lon_cells = spectrum.shape
    tile_count = lax.axis_size("comp")
    tile_width = lon_cells // tile_count
    band_pos = lax.axis_index("band")
    comp_pos = lax.axis_index("comp")
    inverse = jnp.argsort(owner_map)
    gathered = lax.all_gather(currents, "comp", axis=2, tiled=True)
    current_real = reorder_tiles(gathered, inverse, tile_count)
    ocean_pad = jnp.pad(sea_mask.astype(jnp.float32), ((SUBSTEPS, SUBSTEPS), (0, 0)))
    class_pad = jnp.pad(depth_class, ((SUBSTEPS, SUBSTEPS), (0, 0)))
    own_start = band_pos * rows_dev + SUBSTEPS
    ocean_own = lax.dynamic_slice_in_dim(ocean_pad, own_start, rows_dev, 0)
    class_own = lax.dynamic_slice_in_dim(class_pad, own_start, rows_dev, 0)
    weights = stokes_weights(interp.shape[0])
    component = comp_pos * per_device + jnp.arange(per_device, dtype=jnp.int32)
    speeds, cosine, sines, columns = component_tables(component, group_courant, refraction)
    wave_state = spectrum * ocean_own[None]
    lon_speed, lat_speed, dir_speed = coefficients(
        current_real, class_own, speeds, cosine, sines, columns
    )
    for substep in range(SUBSTEPS):
        padded = padded_2(wave_state, (("band", 1),), 1)
        wave_state = advance(padded, lon_speed, lat_speed, dir_speed, ocean_own)
    current_rows = velocity_rows(current_real)
    block_len = rows_dev * lon_cells // tile_count
    blocked = wave_state.reshape(per_device, tile_count, block_len)
    points = lax.all_to_all(blocked, "comp", split_axis=1, concat_axis=0, tiled=True)
    updated, drift_block = source_local(points, interp, weights)
    returned = lax.all_to_all(updated, "comp", split_axis=0, concat_axis=1, tiled=True)
    spectrum_out = returned.reshape(per_device, rows_dev, lon_cells)
    drift_all = lax.all_gather(drift_block, "comp", axis=1, tiled=True).reshape(
        2, rows_dev, lon_cells
    )
    stokes = lax.dynamic_slice_in_dim(drift_all, owner_map[comp_pos] * tile_width, tile_width, 2)
    ocean_rows = lax.dynamic_slice_in_dim(ocean_pad, own_start - 1, rows_dev + 2, 0)
    total_rows = sea_mask.shape[0]
    row_global = band_pos * rows_dev + jnp.arange(rows_dev, dtype=jnp.int32)
    latitude = -1.2 + 2.4 * (row_global.astype(jnp.float32) + 0.5) / total_rows
    coriolis = jnp.sin(latitude)[:, None]
    tile_index = owner_map[comp_pos]
    ocean_out = ocean_update(current_rows, ocean_rows, tile_index, tile_width, stokes, coriolis)
    return (spectrum_out, ocean_out)


def solution(mesh):
    in_specs = (P("comp", "band", None), P(None, "band", "comp"), P(), P(), P(), P(), P(), P())
    out_specs = (P("comp", "band", None), P(None, "band", "comp"))
    return jax.shard_map(local, mesh=mesh, in_specs=in_specs, out_specs=out_specs, check_vma=False)
```

profile of v0, /device:TPU:0, one launch (start us, length us, event | category | flops | bytes accessed | tf_op | source)
XLA Modules:
  0.0 1831.0 jit_solution(6562481310274997737)
XLA Ops:
  33.4 25.7 %fusion.116 = (f32[4,35,8,4096]{3,2,1,0:T(8,128)}, f32[4,35,8,4096]{3,2,1,0:T(8,128)}) fusion(f32[4,36,8,4096]{3,2,1,0:T(8,128)} %bitcast.171), kind=kLoop, calls=%fused_computation.220 | loop fusion | bytes 73400320 | tf_op jit(solution)/shard_map/jit(_roll_static)/slice | solution.py:61
  61.6 31.9 %all_gather.6 = f32[2,8,4096]{2,1,0:T(8,128)S(1)} all-gather(f32[2,8,512]{2,1,0:T(8,128)S(1)} %copy-done.26), channel_id=1, replica_groups=mesh['comp'=8,'band'=4] {'comp'}, dimensions={2}, use_global_device_ids=true | all-gather | bytes 294912 | tf_op jit(solution)/shard_map/all_gather | solution.py:186
  96.0 27.0 %pad_maximum_fusion.8 = (f32[4,36,8,4096]{3,2,1,0:T(8,128)}, f32[4,36,8,4096]{3,2,1,0:T(8,128)}) fusion(f32[4,35,8,4096]{3,2,1,0:T(8,128)} %get-tuple-element.50, f32[4,1,8,4096]{3,2,1,0:T(8,128)} %get-tuple-element.48, f32[4,1,8,4096]{3,2,1,0:T(8,128)} %get-tuple-element.49, f32[4,35,8,4096]{3,2,1,0:T(8,128)} %get-tuple-element.51), kind=kLoop, calls=%fused_computation.65 | loop fusion | flops 9437184 | bytes 75497472 | tf_op jit(solution)/shard_map/jit(_roll_static)/concatenate | solution.py:61
  125.8 13.7 fusion.117
  139.7 46.1 %fusion.20 = f32[144,8,4096]{2,1,0:T(8,128)} fusion(f32[144,8,4096]{2,1,0:T(8,128)S(1)} %bitcast.173, f32[144,1,4096]{2,1,0:T(1,128)} %collective-permute-done.1, f32[144,1,4096]{2,1,0:T(1,128)} %collective-permute-done, f32[144,8,4095]{2,1,0:T(8,128)} %get-tuple-element.53, f32[144,8,1]{2,1,0:T(8,128)S(1)} %copy-done.22, f32[144,8,1]{2,1,0:T(8,128)S(1)} %copy-done.21, ...), kind=kLoop, calls=%fused_computation.27 | loop fusion | flops 221773824 | bytes 119412928 | tf_op jit(solution)/shard_map/mul | solution.py:83
  185.8 17.1 fusion.114
  204.2 25.8 %fusion.111 = (f32[4,35,8,4096]{3,2,1,0:T(8,128)}, f32[4,35,8,4096]{3,2,1,0:T(8,128)}) fusion(f32[4,36,8,4096]{3,2,1,0:T(8,128)} %bitcast.177), kind=kLoop, calls=%fused_computation.215 | loop fusion | bytes 73400320 | tf_op jit(solution)/shard_map/jit(_roll_static)/slice | solution.py:61
  234.5 14.8 pad_maximum_fusion.10
  249.3 14.3 pad_maximum_fusion.11
  263.9 13.7 fusion.112
  277.7 46.3 %fusion.25 = f32[144,8,4096]{2,1,0:T(8,128)} fusion(f32[144,8,4096]{2,1,0:T(8,128)S(1)} %bitcast.179, f32[144,1,4096]{2,1,0:T(1,128)} %collective-permute-done.3, f32[144,1,4096]{2,1,0:T(1,128)} %collective-permute-done.2, f32[144,8,4095]{2,1,0:T(8,128)} %get-tuple-element.43, f32[144,8,1]{2,1,0:T(8,128)S(1)} %get-tuple-element.45, ...), kind=kLoop, calls=%fused_computation.32 | loop fusion | flops 221773824 | bytes 119412928 | tf_op jit(solution)/shard_map/mul | solution.py:83
  324.0 17.2 fusion.109
  342.5 25.8 %fusion.106 = (f32[4,35,8,4096]{3,2,1,0:T(8,128)}, f32[4,35,8,4096]{3,2,1,0:T(8,128)}) fusion(f32[4,36,8,4096]{3,2,1,0:T(8,128)} %bitcast.181), kind=kLoop, calls=%fused_computation.210 | loop fusion | bytes 73400320 | tf_op jit(solution)/shard_map/jit(_roll_static)/slice | solution.py:61
  375.2 14.8 pad_maximum_fusion.12
  390.0 14.3 pad_maximum_fusion.13
  404.5 13.7 fusion.107
  418.2 52.5 %fusion.30 = f32[144,8,4096]{2,1,0:T(8,128)S(1)} fusion(f32[144,8,4096]{2,1,0:T(8,128)} %fusion.25, f32[144,1,4096]{2,1,0:T(1,128)} %collective-permute-done.5, f32[144,1,4096]{2,1,0:T(1,128)} %collective-permute-done.4, f32[144,8,4095]{2,1,0:T(8,128)} %get-tuple-element.33, f32[144,8,1]{2,1,0:T(8,128)S(1)} %get-tuple-element.35, ...), kind=kLoop, calls=%fused_computation.37 | loop fusion | flops 221773824 | bytes 119412928 | tf_op jit(solution)/shard_map/mul | solution.py:83
  495.1 12.7 pad_maximum_fusion.14
  507.7 12.6 pad_maximum_fusion.15
  520.6 13.7 fusion.102
  534.3 46.3 %fusion.35 = f32[144,8,4096]{2,1,0:T(8,128)} fusion(f32[144,8,4096]{2,1,0:T(8,128)S(1)} %fusion.30, f32[144,1,4096]{2,1,0:T(1,128)} %collective-permute-done.7, f32[144,1,4096]{2,1,0:T(1,128)} %collective-permute-done.6, f32[144,8,4095]{2,1,0:T(8,128)} %get-tuple-element.23, f32[144,8,1]{2,1,0:T(8,128)S(1)} %get-tuple-element.25, ...), kind=kLoop, calls=%fused_computation.42 | loop fusion | flops 221773824 | bytes 119412928 | tf_op jit(solution)/shard_map/mul | solution.py:83
  580.6 17.0 copy.27
  597.6 415.9 %all_to_all.33 = f32[144,8,4096]{2,0,1:T(8,128)} all-to-all(f32[144,8,4096]{2,0,1:T(8,128)S(1)} %copy.27), channel_id=1, replica_groups=mesh['comp'=8,'band'=4] {'comp'}, dimensions={1} | all-to-all | bytes 37748736 | tf_op jit(solution)/shard_map/all_to_all | solution.py:206
  1013.4 18.6 %copy.29 = f32[1152,4096]{0,1:T(8,128)} copy(f32[1152,4096]{1,0:T(8,128)} %bitcast.186) | data formatting | bytes 37748736 | tf_op jit(solution)/shard_map/reshape | solution.py:125
  1032.1 99.0 %fusion.123 = f32[4096,1152]{1,0:T(8,128)} fusion(f32[1152,4096]{1,0:T(8,128)} %bitcast.187, f32[1152,1152]{1,0:T(8,128)} %param.12), kind=kOutput, calls=%fused_computation.227 | convolution fusion | flops 65229815808 | bytes 43057152 | tf_op jit(solution)/shard_map/dot_general | solution.py:127
  1131.1 159.0 %fusion.122 = f32[4096,1152]{1,0:T(8,128)} fusion(f32[1152,4096]{1,0:T(8,128)} %bitcast.188, f32[1152,1152]{1,0:T(8,128)} %param.12), kind=kOutput, calls=%fused_computation.226 | convolution fusion | flops 65229815808 | bytes 43057152 | tf_op jit(solution)/shard_map/dot_general | solution.py:126
  1290.1 20.3 %fusion.99 = f32[1152,1,4096]{0,2,1:T(8,128)} fusion(f32[1152,4096]{0,1:T(8,128)S(1)} %bitcast.185, f32[4096,1152]{1,0:T(8,128)} %fusion.122, f32[4096,1152]{1,0:T(8,128)} %fusion.123), kind=kLoop, calls=%fused_computation.203 | loop fusion | flops 33030144 | bytes 75497472 | tf_op jit(solution)/shard_map/reshape | solution.py:139
  1310.4 41.9 %copy.30 = f32[1152,1,4096]{2,1,0:T(1,128)} copy(f32[1152,1,4096]{0,2,1:T(8,128)} %fusion.99) | data formatting | bytes 37748736 | tf_op jit(solution)/shard_map/reshape | solution.py:139
  1364.7 25.5 %fusion.82 = f32[2,4096]{1,0:T(2,128)S(1)} fusion(f32[1,1152]{1,0:T(1,128)S(1)} %get-tuple-element.83, f32[1,1152]{1,0:T(1,128)S(1)} %get-tuple-element.84, f32[1152,4096]{0,1:T(8,128)} %copy.29, f32[4096,1152]{1,0:T(8,128)} %fusion.122, f32[4096,1152]{1,0:T(8,128)} %fusion.123), kind=kOutput, calls=%fused_computation.166 | convolution fusion | flops 146278656 | bytes 56665088 | tf_op jit(solution)/shard_map/dot_general | solution.py:137
  1390.1 396.8 %all-gather = f32[2,32768]{1,0:T(2,128)S(1)} all-gather(f32[2,4096]{1,0:T(2,128)S(1)} %fusion.82), channel_id=2, replica_groups=mesh['comp'=8,'band'=4] {'comp'}, dimensions={1}, use_global_device_ids=true | all-gather | bytes 294912 | tf_op jit(solution)/shard_map/all_gather | solution.py:210
  1787.8 21.2 %copy.33 = f32[1152,1,4096]{2,0,1:T(8,128)S(1)} copy(f32[1152,1,4096]{2,1,0:T(1,128)} %all-to-all-done.1) | data formatting | bytes 37748736
  1809.0 21.8 %copy.32 = f32[144,8,4096]{2,1,0:T(8,128)} copy(f32[144,8,4096]{2,0,1:T(8,128)S(1)} %bitcast.189) | data formatting | bytes 37748736
  (182 shorter events, 91.9 us)
Async XLA Ops:
  0.6 58.6 %copy-start = (f32[32]{0:T(128)S(1)}, f32[32]{0:T(128)}, u32[]{:S(2)}) copy-start(f32[32]{0:T(128)} %param.10) | copy-start | bytes 388
  22.4 117.2 %collective-permute-start = (f32[144,1,4096]{2,1,0:T(1,128)}, f32[144,1,4096]{2,1,0:T(1,128)}, u32[]{:S(2)}, u32[]{:S(2)}) collective-permute-start(f32[144,1,4096]{2,1,0:T(1,128)} %get-tuple-element.56), channel_id=1, source_target_pairs={{0,1},{1,2},{2,3},{4,5},{5,6},{6,7},{8,9},{9,10},{10,11},{12,13},{... | collective-permute-start | bytes 7077896 | tf_op jit(solution)/shard_map/ppermute | solution.py:39
  26.4 113.2 %collective-permute-start.1 = (f32[144,1,4096]{2,1,0:T(1,128)}, f32[144,1,4096]{2,1,0:T(1,128)}, u32[]{:S(2)}, u32[]{:S(2)}) collective-permute-start(f32[144,1,4096]{2,1,0:T(1,128)} %get-tuple-element.57), channel_id=1, source_target_pairs={{1,0},{2,1},{3,2},{5,4},{6,5},{7,6},{9,8},{10,9},{11,10},{13,12},{... | collective-permute-start | bytes 7077896 | tf_op jit(solution)/shard_map/ppermute | solution.py:40
  28.6 65.4 %copy-start.28 = (pred[8]{0:T(512)(128)(4,1)}, pred[8]{0:T(512)(128)(4,1)S(1)}, u32[]{:S(2)}) copy-start(pred[8]{0:T(512)(128)(4,1)S(1)} %compare_and_fusion) | copy-start | bytes 28
  33.4 27.4 %copy-start.27 = (f32[8,32]{1,0:T(8,128)S(1)}, f32[8,32]{1,0:T(8,128)}, u32[]{:S(2)}) copy-start(f32[8,32]{1,0:T(8,128)} %param.11) | copy-start | bytes 3076
  33.4 28.1 %copy-start.26 = (f32[2,8,512]{2,1,0:T(8,128)S(1)}, f32[2,8,512]{2,1,0:T(8,128)}, u32[]{:S(2)}) copy-start(f32[2,8,512]{2,1,0:T(8,128)} %param.9) | copy-start | bytes 98308
  33.4 61.5 %copy-start.25 = (s32[32,4096]{1,0:T(8,128)S(1)}, s32[32,4096]{1,0:T(8,128)}, u32[]{:S(2)}) copy-start(s32[32,4096]{1,0:T(8,128)} %param.14) | copy-start | bytes 1572868
  94.9 28.6 %slice-start = ((s8[18874368]{0:T(1024)(128)(4,1)}), s8[4194304]{0:T(1024)(128)(4,1)S(1)}, s32[]{:S(2)}) async-start(s8[18874368]{0:T(1024)(128)(4,1)} %bitcast.172), calls=%async_computation.2 | async-start | bytes 8388608
  95.9 27.5 %slice-start.1 = ((s8[18874368]{0:T(1024)(128)(4,1)}), s8[4194304]{0:T(1024)(128)(4,1)S(1)}, s32[]{:S(2)}) async-start(s8[18874368]{0:T(1024)(128)(4,1)} %bitcast.172), calls=%async_computation.3 | async-start | bytes 8388608
  96.0 27.6 %slice-start.2 = ((s8[18874368]{0:T(1024)(128)(4,1)}), s8[4194304]{0:T(1024)(128)(4,1)S(1)}, s32[]{:S(2)}) async-start(s8[18874368]{0:T(1024)(128)(4,1)} %bitcast.172), calls=%async_computation.4 | async-start | bytes 8388608
  96.0 29.2 %slice-start.3 = ((s8[18874368]{0:T(1024)(128)(4,1)}), s8[4194304]{0:T(1024)(128)(4,1)S(1)}, s32[]{:S(2)}) async-start(s8[18874368]{0:T(1024)(128)(4,1)} %bitcast.172), calls=%async_computation.5 | async-start | bytes 8388608
  96.0 29.8 %slice-start.4 = ((s8[18874368]{0:T(1024)(128)(4,1)}), s8[2097152]{0:T(1024)(128)(4,1)S(1)}, s32[]{:S(2)}) async-start(s8[18874368]{0:T(1024)(128)(4,1)} %bitcast.172), calls=%async_computation.6 | async-start | bytes 4194304
  229.9 47.7 %collective-permute-start.2 = (f32[144,1,4096]{2,1,0:T(1,128)}, f32[144,1,4096]{2,1,0:T(1,128)}, u32[]{:S(2)}, u32[]{:S(2)}) collective-permute-start(f32[144,1,4096]{2,1,0:T(1,128)} %get-tuple-element.46), channel_id=1, source_target_pairs={{0,1},{1,2},{2,3},{4,5},{5,6},{6,7},{8,9},{9,10},{10,11},{12,13},{... | collective-permute-start | bytes 7077896 | tf_op jit(solution)/shard_map/ppermute | solution.py:39
  232.8 44.8 %collective-permute-start.3 = (f32[144,1,4096]{2,1,0:T(1,128)S(1)}, f32[144,1,4096]{2,1,0:T(1,128)}, u32[]{:S(2)}, u32[]{:S(2)}) collective-permute-start(f32[144,1,4096]{2,1,0:T(1,128)S(1)} %get-tuple-element.47), channel_id=1, source_target_pairs={{1,0},{2,1},{3,2},{5,4},{6,5},{7,6},{9,8},{10,9},{11,10},{13,12},{... | collective-permute-start | bytes 7077896 | tf_op jit(solution)/shard_map/ppermute | solution.py:40
  234.5 29.1 %slice-start.5 = ((s8[18874368]{0:T(1024)(128)(4,1)}), s8[4194304]{0:T(1024)(128)(4,1)S(1)}, s32[]{:S(2)}) async-start(s8[18874368]{0:T(1024)(128)(4,1)} %bitcast.178), calls=%async_computation.7 | async-start | bytes 8388608
  234.5 29.1 %slice-start.6 = ((s8[18874368]{0:T(1024)(128)(4,1)}), s8[4194304]{0:T(1024)(128)(4,1)S(1)}, s32[]{:S(2)}) async-start(s8[18874368]{0:T(1024)(128)(4,1)} %bitcast.178), calls=%async_computation.8 | async-start | bytes 8388608
  234.5 29.0 %slice-start.7 = ((s8[18874368]{0:T(1024)(128)(4,1)}), s8[4194304]{0:T(1024)(128)(4,1)S(1)}, s32[]{:S(2)}) async-start(s8[18874368]{0:T(1024)(128)(4,1)} %bitcast.178), calls=%async_computation.9 | async-start | bytes 8388608
  368.3 49.9 %collective-permute-start.4 = (f32[144,1,4096]{2,1,0:T(1,128)}, f32[144,1,4096]{2,1,0:T(1,128)}, u32[]{:S(2)}, u32[]{:S(2)}) collective-permute-start(f32[144,1,4096]{2,1,0:T(1,128)} %get-tuple-element.36), channel_id=1, source_target_pairs={{0,1},{1,2},{2,3},{4,5},{5,6},{6,7},{8,9},{9,10},{10,11},{12,13},{... | collective-permute-start | bytes 7077896 | tf_op jit(solution)/shard_map/ppermute | solution.py:39
  373.9 44.3 %collective-permute-start.5 = (f32[144,1,4096]{2,1,0:T(1,128)S(1)}, f32[144,1,4096]{2,1,0:T(1,128)}, u32[]{:S(2)}, u32[]{:S(2)}) collective-permute-start(f32[144,1,4096]{2,1,0:T(1,128)S(1)} %get-tuple-element.37), channel_id=1, source_target_pairs={{1,0},{2,1},{3,2},{5,4},{6,5},{7,6},{9,8},{10,9},{11,10},{13,12},{... | collective-permute-start | bytes 7077896 | tf_op jit(solution)/shard_map/ppermute | solution.py:40
  375.2 29.1 %slice-start.10 = ((s8[18874368]{0:T(1024)(128)(4,1)}), s8[4194304]{0:T(1024)(128)(4,1)S(1)}, s32[]{:S(2)}) async-start(s8[18874368]{0:T(1024)(128)(4,1)} %bitcast.182), calls=%async_computation.12 | async-start | bytes 8388608
  375.2 29.0 %slice-start.11 = ((s8[18874368]{0:T(1024)(128)(4,1)}), s8[4194304]{0:T(1024)(128)(4,1)S(1)}, s32[]{:S(2)}) async-start(s8[18874368]{0:T(1024)(128)(4,1)} %bitcast.182), calls=%async_computation.13 | async-start | bytes 8388608
  375.2 29.0 %slice-start.12 = ((s8[18874368]{0:T(1024)(128)(4,1)}), s8[4194304]{0:T(1024)(128)(4,1)S(1)}, s32[]{:S(2)}) async-start(s8[18874368]{0:T(1024)(128)(4,1)} %bitcast.182), calls=%async_computation.14 | async-start | bytes 8388608
  489.0 45.2 %collective-permute-start.6 = (f32[144,1,4096]{2,1,0:T(1,128)}, f32[144,1,4096]{2,1,0:T(1,128)}, u32[]{:S(2)}, u32[]{:S(2)}) collective-permute-start(f32[144,1,4096]{2,1,0:T(1,128)} %get-tuple-element.26), channel_id=1, source_target_pairs={{0,1},{1,2},{2,3},{4,5},{5,6},{6,7},{8,9},{9,10},{10,11},{12,13},{... | collective-permute-start | bytes 7077896 | tf_op jit(solution)/shard_map/ppermute | solution.py:39
  493.6 40.7 %collective-permute-start.7 = (f32[144,1,4096]{2,1,0:T(1,128)S(1)}, f32[144,1,4096]{2,1,0:T(1,128)}, u32[]{:S(2)}, u32[]{:S(2)}) collective-permute-start(f32[144,1,4096]{2,1,0:T(1,128)S(1)} %get-tuple-element.27), channel_id=1, source_target_pairs={{1,0},{2,1},{3,2},{5,4},{6,5},{7,6},{9,8},{10,9},{11,10},{13,12},{... | collective-permute-start | bytes 7077896 | tf_op jit(solution)/shard_map/ppermute | solution.py:40
  1032.1 258.0 %slice-start.15 = ((s8[18874368]{0:T(1024)(128)(4,1)}), s8[4194304]{0:T(1024)(128)(4,1)S(1)}, s32[]{:S(2)}) async-start(s8[18874368]{0:T(1024)(128)(4,1)} %bitcast.184), calls=%async_computation.17 | async-start | bytes 8388608
  1032.1 258.0 %slice-start.16 = ((s8[18874368]{0:T(1024)(128)(4,1)}), s8[4194304]{0:T(1024)(128)(4,1)S(1)}, s32[]{:S(2)}) async-start(s8[18874368]{0:T(1024)(128)(4,1)} %bitcast.184), calls=%async_computation.18 | async-start | bytes 8388608
  1032.1 258.0 %slice-start.17 = ((s8[18874368]{0:T(1024)(128)(4,1)}), s8[4194304]{0:T(1024)(128)(4,1)S(1)}, s32[]{:S(2)}) async-start(s8[18874368]{0:T(1024)(128)(4,1)} %bitcast.184), calls=%async_computation.19 | async-start | bytes 8388608
  1131.1 159.0 %slice-start.18 = ((s8[18874368]{0:T(1024)(128)(4,1)}), s8[4194304]{0:T(1024)(128)(4,1)S(1)}, s32[]{:S(2)}) async-start(s8[18874368]{0:T(1024)(128)(4,1)} %bitcast.184), calls=%async_computation.20 | async-start | bytes 8388608
  1131.1 159.0 %slice-start.19 = ((s8[18874368]{0:T(1024)(128)(4,1)}), s8[2097152]{0:T(1024)(128)(4,1)S(1)}, s32[]{:S(2)}) async-start(s8[18874368]{0:T(1024)(128)(4,1)} %bitcast.184), calls=%async_computation.21 | async-start | bytes 4194304
  1352.3 435.5 %all-to-all-start.1 = ((f32[1152,1,4096]{2,1,0:T(1,128)}), f32[1152,1,4096]{2,1,0:T(1,128)}, u32[]{:S(2)}, u32[]{:S(2)}) async-start(f32[1152,1,4096]{2,1,0:T(1,128)} %copy.30), calls=%async_computation.1 | async-start | bytes 37748736 | tf_op jit(solution)/shard_map/all_to_all | solution.py:208
  1358.6 5.1 collective-permute-start.8
  1360.5 3.5 collective-permute-start.9
  (31 other events, 401.4 us)
where the time goes:
time: 1840 us; the launch traced here: 1830 us
  blocking collectives  845 us (46%)
  other arithmetic  335 us (18%)
  local copies, waits for them, and re-layouts  334 us (18%)
  matrix products  283 us (15%)
  starting transfers between devices  31.9 us (2%)
    all_to_all x1, blocking collectives, local(): lax.all_to_all(blocked, 'comp', split_axis=1, concat_axis=0, tiled=True)  416 us
    all_gather x1, blocking collectives, local(): lax.all_gather(drift_block, 'comp', axis=1, tiled=True)  397 us
    mul x4, other arithmetic, advance(): return ocean_rows[None] * (centre - change)  191 us
    dot_general x1, matrix products, source_local(): jnp.dot(interp, flat_spec, precision=HIGHEST, preferred_element_type=jnp....  159 us
    dot_general x1, matrix products, source_local(): lax.dot_general(interp, flat_spec, (((0,), (0,)), ((), ())), precision=HI...  99 us
    slice x8, local copies, waits for them, and re-layouts, direction_pair(): before_dir = jnp.roll(circles, 1, axis=1).reshape(centre.shape)  94.6 us
    concatenate x4, other arithmetic, direction_pair(): before_dir = jnp.roll(circles, 1, axis=1).reshape(centre.shape)  69.2 us
    slice x8, local copies, waits for them, and re-layouts, advance(): east_cols = jnp.roll(centre, -1, axis=2)  57.9 us
  transfers between devices with their start and end apart: 11, of which 1 were waited for; matrix products, arithmetic and copies ran while one was open for 13% of the time, Pallas kernels for 0%

commit v1 on v0

--- a/solution.py
+++ b/solution.py
@@ -1,9 +1,13 @@
+import functools
 import math
 
 import jax
 import jax.numpy as jnp
 from jax import lax
+from jax.experimental import pallas as pl
+from jax.experimental.pallas import tpu as pltpu
 from jax.sharding import PartitionSpec as P
+
 
 DIRS = 36
 FREQ = 32
@@ -197,7 +201,7 @@
     lon_speed, lat_speed, dir_speed = coefficients(
         current_real, class_own, speeds, cosine, sines, columns
     )
-    for substep in range(SUBSTEPS):
+    for _ in range(SUBSTEPS):
         padded = padded_2(wave_state, (("band", 1),), 1)
         wave_state = advance(padded, lon_speed, lat_speed, dir_speed, ocean_own)
     current_rows = velocity_rows(current_real)
@@ -221,7 +225,464 @@
     return (spectrum_out, ocean_out)
 
 
+SUBLANES = 8
+LANES = 128
+HALVES = 2
+
+
+def partner_routes(count, step):
+    return [(i, i ^ step) for i in range(count)]
+
+
+def wave_kernel(
+    order_ref, courant_ref, refract_ref, angle_ref, spec_ref, gathered_ref, north_ref, south_ref, ocean_ref, class_ref,
+    *rest, group, groups, pieces, parts
+):
+    outs = rest[:pieces]
+    own_a, halo_a, own_b, halo_b, stage, vel, turn, in_sems, out_sems = rest[pieces:]
+    dirs, rows, width = own_a.shape
+    tiles = width // LANES
+    count = gathered_ref.shape[0]
+    tile_width = width // count
+    per_tile = tile_width // LANES
+    per_part = per_tile // parts
+    me = lax.axis_index("comp")
+    frequency = me * groups + group
+    loads = [pltpu.make_async_copy(spec_ref.at[pl.ds(group * dirs, dirs)], own_a, in_sems.at[0])]
+    for j in range(count):
+        start = pl.multiple_of(order_ref[me ^ j] * tile_width, LANES)
+        loads.append(
+            pltpu.make_async_copy(gathered_ref.at[j], vel.at[:, :, pl.ds(start, tile_width)], in_sems.at[1 + j])
+        )
+    for load in loads:
+        load.start()
+    turning = jnp.zeros(class_ref.shape, jnp.float32)
+    for level in range(refract_ref.shape[0]):
+        turning = jnp.where(class_ref[...] == level, refract_ref[level, frequency], turning)
+    turn[...] = turning
+    for load in loads:
+        load.wait()
+    vel[...] = vel[...] * CURRENT_COURANT
+
+    def enter(d, carry):
+        own_a[d] = own_a[d] * ocean_ref[0:rows, :]
+        halo_a[d] = jnp.concatenate([north_ref[d], south_ref[d]], axis=0) * ocean_ref[rows : 2 * rows, :]
+        return carry
+
+    lax.fori_loop(0, dirs, enter, 0)
+    speed = courant_ref[frequency]
+    lane = lax.broadcasted_iota(jnp.int32, (rows, LANES), 1)
+    row = lax.broadcasted_iota(jnp.int32, (rows, LANES), 0)
+    is_first_lane = lane == 0
+    is_last_lane = lane == LANES - 1
+    is_first_row = row == 0
+    is_last_row = row == rows - 1
+
+    def substep(own, halo, own_next, halo_next, last):
+        def one_direction(d, carry):
+            before = jnp.where(d == 0, dirs - 1, d - 1)
+            after = jnp.where(d == dirs - 1, 0, d + 1)
+            cosine = angle_ref[0, d]
+            speed_x = speed * cosine
+            speed_y = speed * angle_ref[1, d]
+            cache = {}
+
+            def tile_of(field, name, at):
+                key = (name, at)
+                if key not in cache:
+                    value = field[d, :, at * LANES : (at + 1) * LANES]
+                    cache[key] = (value, pltpu.roll(value, 1, 1), pltpu.roll(value, LANES - 1, 1))
+                return cache[key]
+
+            def advanced(field, name, at, south, north, part):
+                value, up, down = tile_of(field, name, at)
+                west = jnp.where(is_first_lane, tile_of(field, name, (at - 1) % tiles)[1], up)
+                east = jnp.where(is_last_lane, tile_of(field, name, (at + 1) % tiles)[2], down)
+                cols = slice(at * LANES, (at + 1) * LANES)
+                span = slice(part * rows, (part + 1) * rows)
+                along = speed_x + vel[0, span, cols]
+                across = speed_y + vel[1, span, cols]
+                turned = turn[span, cols] * cosine
+                ahead = field[after, :, cols]
+                behind = field[before, :, cols]
+                result = value - jnp.abs(along) * (value - jnp.where(along > 0.0, west, east))
+                result = result - jnp.abs(across) * (value - jnp.where(across > 0.0, south, north))
+                result = result - jnp.abs(turned) * (value - jnp.where(turned > 0.0, behind, ahead))
+                return ocean_ref[span, cols] * result
+
+            for at in range(tiles):
+                mine = tile_of(own, "own", at)[0]
+                cols = slice(at * LANES, (at + 1) * LANES)
+                other = halo[d, :, cols]
+                own_up = pltpu.roll(mine, 1, 0)
+                own_down = pltpu.roll(mine, rows - 1, 0)
+                halo_up = pltpu.roll(other, 1, 0)
+                halo_down = pltpu.roll(other, rows - 1, 0)
+                south = jnp.where(is_first_row, halo_up, own_up)
+                north = jnp.where(is_last_row, halo_down, own_down)
+                result = advanced(own, "own", at, south, north, 0)
+                if last:
+                    stage[at // per_tile, at % per_tile, d] = result
+                else:
+                    own_next[d, :, cols] = result
+                    south = jnp.where(is_first_row, own_up, halo_up)
+                    north = jnp.where(is_last_row, own_down, halo_down)
+                    halo_next[d, :, cols] = advanced(halo, "halo", at, south, north, 1)
+            return carry
+
+        lax.fori_loop(0, dirs, one_direction, 0)
+
+    def two_substeps(turn_count, carry):
+        substep(own_a, halo_a, own_b, halo_b, False)
+
+        @pl.when(turn_count < SUBSTEPS // 2 - 1)
+        def _():
+            substep(own_b, halo_b, own_a, halo_a, False)
+
+        return carry
+
+    lax.fori_loop(0, SUBSTEPS // 2, two_substeps, 0)
+    substep(own_b, halo_b, None, None, True)
+    stores = []
+    for k in range(count):
+        tile = order_ref[me ^ k]
+        for part in range(parts):
+            n = k * parts + part
+            stores.append(
+                pltpu.make_async_copy(stage.at[tile, pl.ds(part * per_part, per_part)], outs[n], out_sems.at[n])
+            )
+    for store in stores:
+        store.start()
+    for store in stores:
+        store.wait()
+
+
+def wave_group(
+    owner_map, courant, refraction, angles, spectrum, gathered, north, south, ocean16, class16, group, groups, parts
+):
+    _, rows, width = spectrum.shape
+    count = gathered.shape[0]
+    per_tile = width // count // LANES
+    pieces = count * parts
+    piece = jax.ShapeDtypeStruct((per_tile // parts, DIRS, rows, LANES), jnp.float32)
+    smem = pl.BlockSpec(memory_space=pltpu.SMEM)
+    hbm = pl.BlockSpec(memory_space=pltpu.HBM)
+    vmem = pl.BlockSpec(memory_space=pltpu.VMEM)
+    state = pltpu.VMEM((DIRS, rows, width), jnp.float32)
+    return pl.pallas_call(
+        functools.partial(wave_kernel, group=group, groups=groups, pieces=pieces, parts=parts),
+        out_shape=[piece] * pieces,
+        in_specs=[smem, smem, smem, smem, hbm, hbm, vmem, vmem, vmem, vmem],
+        out_specs=[hbm] * pieces,
+        scratch_shapes=[
+            state,
+            state,
+            state,
+            state,
+            pltpu.VMEM((count, per_tile, DIRS, rows, LANES), jnp.float32),
+            pltpu.VMEM((2, 2 * rows, width), jnp.float32),
+            pltpu.VMEM((2 * rows, width), jnp.float32),
+            pltpu.SemaphoreType.DMA((count + 1,)),
+            pltpu.SemaphoreType.DMA((pieces,)),
+        ],
+        compiler_params=pltpu.CompilerParams(vmem_limit_bytes=48 * 1024 * 1024),
+        cost_estimate=pl.CostEstimate(flops=2_000_000_000, bytes_accessed=20_000_000, transcendentals=0),
+        name="wave_group",
+    )(owner_map, courant, refraction, angles, spectrum, gathered, north, south, ocean16, class16)
+
+
+def source_kernel(high_ref, low_ref, weight_ref, *rest, groups, count, offsets):
+    ins = rest[: count * groups]
+    outs = rest[count * groups : count * groups + count]
+    drift_ref, state, result, x_high, x_low, forward, backward, in_sems, out_sems = rest[count * groups + count :]
+    lane_tiles, comps, rows, _ = state.shape
+    per_device = comps // count
+    per_group = per_device // groups
+    me = lax.axis_index("comp")
+    loads = []
+    for k in range(count):
+        for g in range(groups):
+            n = k * groups + g
+            start = (me ^ k) * per_device + g * per_group
+            loads.append(
+                pltpu.make_async_copy(
+                    ins[n].at[pl.ds(offsets[n], lane_tiles)], state.at[:, pl.ds(start, per_group)], in_sems.at[n]
+                )
+            )
+    for load in loads:
+        load.start()
+    for load in loads:
+        load.wait()
+    for tile in range(lane_tiles):
+        flat = state.at[tile].reshape(comps * rows, LANES)
+        flat_out = result.at[tile].reshape(comps * rows, LANES)
+
+        def row_pair(pair, carry):
+            left = 2 * pair
+            for side in range(2):
+                part = flat[pl.ds(left + side, comps, stride=rows), :]
+                high = part.astype(jnp.bfloat16)
+                cols = slice(side * LANES, (side + 1) * LANES)
+                x_high[:, cols] = high
+                x_low[:, cols] = (part - high.astype(jnp.float32)).astype(jnp.bfloat16)
+            for target, begin in ((forward, 0), (backward, comps)):
+                span = slice(begin, begin + comps)
+                target[...] = (
+                    jnp.dot(high_ref[span, :], x_high[...], preferred_element_type=jnp.float32)
+                    + jnp.dot(high_ref[span, :], x_low[...], preferred_element_type=jnp.float32)
+                    + jnp.dot(low_ref[span, :], x_high[...], preferred_element_type=jnp.float32)
+                )
+            for side in range(2):
+                cols = slice(side * LANES, (side + 1) * LANES)
+                part = flat[pl.ds(left + side, comps, stride=rows), :]
+                ahead = forward[:, cols]
+                back = backward[:, cols]
+                updated = part + SOURCE_STEP * (ahead * back - 0.5 * part * (ahead + back))
+                flat_out[pl.ds(left + side, comps, stride=rows), :] = updated
+                for axis in range(2):
+                    drift_ref[axis, tile, pl.ds(left + side, 1), :] = jnp.sum(
+                        updated * weight_ref[axis], axis=0, keepdims=True
+                    )
+            return carry
+
+        lax.fori_loop(0, rows // 2, row_pair, 0)
+    stores = []
+    for k in range(count):
+        start = (me ^ k) * per_device
+        stores.append(pltpu.make_async_copy(result.at[:, pl.ds(start, per_device)], outs[k], out_sems.at[k]))
+    for store in stores:
+        store.start()
+    for store in stores:
+        store.wait()
+
+
+def source_block(high, low, weights, pieces, offsets, lane_tiles, groups, count):
+    _, per_group, rows, _ = pieces[0].shape
+    per_device = groups * per_group
+    comps = count * per_device
+    hbm = pl.BlockSpec(memory_space=pltpu.HBM)
+    vmem = pl.BlockSpec(memory_space=pltpu.VMEM)
+    *outs, drift = pl.pallas_call(
+        functools.partial(source_kernel, groups=groups, count=count, offsets=offsets),
+        out_shape=[jax.ShapeDtypeStruct((lane_tiles, per_device, rows, LANES), jnp.float32)] * count
+        + [jax.ShapeDtypeStruct((2, lane_tiles, rows, LANES), jnp.float32)],
+        in_specs=[vmem, vmem, vmem] + [hbm] * (count * groups),
+        out_specs=[hbm] * count + [vmem],
+        scratch_shapes=[
+            pltpu.VMEM((lane_tiles, comps, rows, LANES), jnp.float32),
+            pltpu.VMEM((lane_tiles, comps, rows, LANES), jnp.float32),
+            pltpu.VMEM((comps, 2 * LANES), jnp.bfloat16),
+            pltpu.VMEM((comps, 2 * LANES), jnp.bfloat16),
+            pltpu.VMEM((comps, 2 * LANES), jnp.float32),
+            pltpu.VMEM((comps, 2 * LANES), jnp.float32),
+            pltpu.SemaphoreType.DMA((count * groups,)),
+            pltpu.SemaphoreType.DMA((count,)),
+        ],
+        compiler_params=pltpu.CompilerParams(vmem_limit_bytes=56 * 1024 * 1024),
+        cost_estimate=pl.CostEstimate(flops=4_000_000_000, bytes_accessed=40_000_000, transcendentals=0),
+        name="source_block",
+    )(high, low, weights, *pieces)
+    return outs, drift
+
+
+def place_kernel(order_ref, *rest, count, half, seeded):
+    ins = rest[:count]
+    out_ref, stage, in_sems, out_sems = rest[count + seeded :]
+    lane_tiles = ins[0].shape[0]
+    me = lax.axis_index("comp")
+    tile_width = out_ref.shape[2] // count
+    loads = [pltpu.make_async_copy(ins[k], stage.at[k], in_sems.at[k]) for k in range(count)]
+    for load in loads:
+        load.start()
+    stores = []
+    for k in range(count):
+        loads[k].wait()
+        for tile in range(lane_tiles):
+            start = order_ref[me ^ k] * tile_width + (half * lane_tiles + tile) * LANES
+            stores.append(
+                pltpu.make_async_copy(
+                    stage.at[k, tile],
+                    out_ref.at[:, :, pl.ds(pl.multiple_of(start, LANES), LANES)],
+                    out_sems.at[k * lane_tiles + tile],
+                )
+            )
+            stores[-1].start()
+    for store in stores:
+        store.wait()
+
+
+def place_half(owner_map, pieces, target, half, width):
+    lane_tiles, per_device, rows, _ = pieces[0].shape
+    count = len(pieces)
+    seeded = int(target is not None)
+    hbm = pl.BlockSpec(memory_space=pltpu.HBM)
+    return pl.pallas_call(
+        functools.partial(place_kernel, count=count, half=half, seeded=seeded),
+        out_shape=jax.ShapeDtypeStruct((per_device, rows, width), jnp.float32),
+        in_specs=[pl.BlockSpec(memory_space=pltpu.SMEM)] + [hbm] * (count + seeded),
+        out_specs=hbm,
+        scratch_shapes=[
+            pltpu.VMEM((count, lane_tiles, per_device, rows, LANES), jnp.float32),
+            pltpu.SemaphoreType.DMA((count,)),
+            pltpu.SemaphoreType.DMA((count * lane_tiles,)),
+        ],
+        input_output_aliases={1 + count: 0} if seeded else {},
+        name="place_half",
+    )(owner_map, *pieces, *([target] if seeded else []))
+
+
+def band_rows(value, dim):
+    count, length = (lax.axis_size("band"), value.shape[dim])
+    up = [(i, i + 1) for i in range(count - 1)]
+    down = [(j, i) for i, j in up]
+    last = lax.slice_in_dim(value, length - SUBSTEPS, length, axis=dim)
+    first = lax.slice_in_dim(value, 0, SUBSTEPS, axis=dim)
+    north = lax.ppermute(first, "band", down)
+    south = lax.ppermute(last, "band", up)
+    return north, south
+
+
+def local_fused(spectrum, currents, group_courant, refraction, interp, sea_mask, depth_class, owner_map):
+    per_device, rows, width = spectrum.shape
+    count = lax.axis_size("comp")
+    tile_width = width // count
+    groups = per_device // DIRS
+    band_pos = lax.axis_index("band")
+    comp_pos = lax.axis_index("comp")
+    north_cur, south_cur = band_rows(currents, 1)
+    stacked = jnp.concatenate([currents, north_cur, south_cur], axis=1)
+    gathered = stacked[None]
+    step = 1
+    while step < count:
+        gathered = jnp.concatenate([gathered, lax.ppermute(gathered, "comp", partner_routes(count, step))], axis=0)
+        step *= 2
+    halo = band_rows(spectrum[:DIRS], 1)
+
+    def sixteen(field):
+        padded = jnp.pad(field, ((SUBSTEPS, SUBSTEPS), (0, 0)))
+        window = lax.dynamic_slice_in_dim(padded, band_pos * rows, rows + 2 * SUBSTEPS, 0)
+        return jnp.concatenate(
+            [window[SUBSTEPS : SUBSTEPS + rows], window[SUBSTEPS + rows :], window[:SUBSTEPS]], axis=0
+        )
+
+    ocean16 = sixteen(sea_mask.astype(jnp.float32))
+    class16 = sixteen(depth_class)
+    angles = jnp.arange(DIRS, dtype=jnp.int32).astype(jnp.float32) * (2.0 * math.pi / DIRS)
+    angles = jnp.stack([jnp.cos(angles), jnp.sin(angles)])
+    steps = list(range(1, count))
+    received = {}
+    waiting = {}
+
+    def send(g, part, k, piece):
+        received[k, g, part] = lax.ppermute(piece, "comp", partner_routes(count, k))
+
+    source = spectrum
+    for g in range(groups):
+        parts = parts_of(g)
+        pieces = wave_group(
+            owner_map, group_courant, refraction, angles, spectrum, gathered, *halo, ocean16, class16, g, groups, parts
+        )
+        interp, source, pieces = lax.optimization_barrier((interp, source, pieces))
+        if g < groups - 1:
+            halo = band_rows(source[(g + 1) * DIRS : (g + 2) * DIRS], 1)
+        for part in range(parts):
+            received[0, g, part] = pieces[part]
+        for k in steps:
+            send(g, 0, k, pieces[k * parts])
+            for part in range(1, parts):
+                waiting[g, part, k] = pieces[k * parts + part]
+    waiting, pieces = lax.optimization_barrier((waiting, pieces))
+    for (g, part, k), piece in waiting.items():
+        send(g, part, k, piece)
+    stacked_interp = jnp.concatenate([interp, interp.T], axis=0)
+    rounded = lax.reduce_precision(stacked_interp, 8, 7)
+    high = rounded.astype(jnp.bfloat16)
+    low = (stacked_interp - rounded).astype(jnp.bfloat16)
+    weights = jnp.broadcast_to(stokes_weights(interp.shape[0])[:, :, None], (2, interp.shape[0], LANES))
+    lane_tiles = tile_width // LANES // HALVES
+    spectrum_out = None
+    drifts = []
+    returned = []
+    for half in range(HALVES):
+        blocks, offsets = [], []
+        for k in range(count):
+            for g in range(groups):
+                split = (k, g, 1) in received
+                blocks.append(received[k, g, half if split else 0])
+                offsets.append(0 if split else half * lane_tiles)
+        outs, drift = source_block(high, low, weights, blocks, offsets, lane_tiles, groups, count)
+        drifts.append(drift)
+        returned.append(
+            [outs[0]] + [lax.ppermute(outs[k], "comp", partner_routes(count, k)) for k in steps]
+        )
+    for half in range(HALVES):
+        spectrum_out = place_half(owner_map, returned[half], spectrum_out, half, width)
+    stokes = jnp.concatenate(drifts, axis=1).transpose(0, 2, 1, 3).reshape(2, rows, tile_width)
+    tile_index = owner_map[comp_pos]
+    order = owner_map[comp_pos ^ jnp.arange(count, dtype=jnp.int32)]
+    last_cols = gathered[:, :, :, -1]
+    first_cols = gathered[:, :, :, 0]
+
+    def picked(cols, tile):
+        chosen = (order == tile % count)[:, None, None]
+        return jnp.sum(jnp.where(chosen, cols, 0.0), axis=0)[:, :, None]
+
+    around = jnp.concatenate(
+        [picked(last_cols, tile_index + count - 1), stacked, picked(first_cols, tile_index + 1)], axis=2
+    )
+    wrapped = jnp.concatenate([ocean16[:, -1:], ocean16, ocean16[:, :1]], axis=1)
+    sea = lax.dynamic_slice_in_dim(wrapped, tile_index * tile_width, tile_width + 2, 1)
+    masked = around * sea[None]
+    extended = jnp.concatenate(
+        [masked[:, 2 * rows - 1 :], masked[:, :rows], masked[:, rows : rows + 1]], axis=1
+    )
+    centre = extended[:, 1:-1, 1:-1]
+    laplace = (
+        extended[:, 1:-1, :-2]
+        + extended[:, 1:-1, 2:]
+        + extended[:, :-2, 1:-1]
+        + extended[:, 2:, 1:-1]
+        - 4.0 * centre
+    )
+    sea_tile = sea[:rows, 1:-1]
+    row_global = band_pos * rows + jnp.arange(rows, dtype=jnp.int32)
+    latitude = -1.2 + 2.4 * (row_global.astype(jnp.float32) + 0.5) / sea_mask.shape[0]
+    coriolis = jnp.sin(latitude)[:, None]
+    east_new = sea_tile * (
+        centre[0]
+        + OCEAN_STEP * (coriolis * (centre[1] + stokes[1]) + VISCOSITY * laplace[0] - DRAG * centre[0])
+    )
+    north_new = sea_tile * (
+        centre[1]
+        + OCEAN_STEP * (-coriolis * (centre[0] + stokes[0]) + VISCOSITY * laplace[1] - DRAG * centre[1])
+    )
+    return (spectrum_out, jnp.stack([east_new, north_new]))
+
+
+def parts_of(group):
+    return 1 if group == 0 else HALVES
+
+
+def fits(mesh, spectrum):
+    comps, rows_all, width = spectrum.shape
+    count = mesh.shape["comp"]
+    return (
+        (comps // count) % DIRS == 0
+        and count & (count - 1) == 0
+        and rows_all // mesh.shape["band"] == SUBLANES
+        and width % (count * HALVES * LANES) == 0
+    )
+
+
 def solution(mesh):
     in_specs = (P("comp", "band", None), P(None, "band", "comp"), P(), P(), P(), P(), P(), P())
     out_specs = (P("comp", "band", None), P(None, "band", "comp"))
-    return jax.shard_map(local, mesh=mesh, in_specs=in_specs, out_specs=out_specs, check_vma=False)
+    shard = functools.partial(jax.shard_map, mesh=mesh, in_specs=in_specs, out_specs=out_specs, check_vma=False)
+
+    def step(spectrum, *others):
+        if not fits(mesh, spectrum):
+            return shard(local)(spectrum, *others)
+
+        return shard(local_fused)(spectrum, *others)
+
+    return step

time: 1840 us -> 1250 us (0.68)
  the two profiles are of different devices: /device:TPU:0 before, /device:TPU:8 now
where the time goes in v1:
time: 1250 us; the launch traced here: 1240 us
  waiting for transfers between devices  638 us (51%)
  Pallas kernels  301 us (24%)
  starting transfers between devices  230 us (18%)
  local copies, waits for them, and re-layouts  50.3 us (4%)
  other arithmetic  14.4 us (1%)
    ppermute x49, waiting for transfers between devices, send(): received[k, g, part] = lax.ppermute(piece, 'comp', partner_routes(count, k))  333 us
    ppermute x14, waiting for transfers between devices, local_fused(): lax.ppermute(outs[k], 'comp', partner_routes(count, k))  277 us
    pallas_call x4, Pallas kernels, wave_group(): pl.pallas_call(functools.partial(wave_kernel, group=group, groups=groups,...  175 us
    pallas_call x2, Pallas kernels, source_block(): pl.pallas_call(functools.partial(source_kernel, groups=groups, count=coun...  110 us
    ppermute x49, starting transfers between devices, send(): received[k, g, part] = lax.ppermute(piece, 'comp', partner_routes(count, k))  91.9 us
    ppermute x14, starting transfers between devices, local_fused(): lax.ppermute(outs[k], 'comp', partner_routes(count, k))  66.5 us
    ppermute x5, starting transfers between devices, band_rows(): south = lax.ppermute(last, 'band', up)  60.3 us
  transfers between devices with their start and end apart: 76, of which 39 were waited for; matrix products, arithmetic and copies ran while one was open for 3% of the time, Pallas kernels for 13%

profile of v1, /device:TPU:8, one launch (start us, length us, event | category | flops | bytes accessed | tf_op | source)
XLA Modules:
  0.0 1237.8 jit_solution(8036851227720772484)
XLA Ops:
  35.3 10.4 collective-permute-done.4
  47.2 43.8 %wave_group.4 = (f32[4,36,8,128]{3,2,1,0:T(8,128)S(1)}, f32[4,36,8,128]{3,2,1,0:T(8,128)S(1)}, f32[4,36,8,128]{3,2,1,0:T(8,128)S(1)}, f32[4,36,8,128]{3,2,1,0:T(...) custom-call(s32[8]{0:T(128)S(1)} %copy-done, ...), custom_call_target="tpu_custom_call" | custom-call | flops 2000000000 | bytes 20000000 | tf_op jit(solution)/shard_map/wave_group/pallas_call | solution.py:372
  104.8 43.9 %wave_group.5 = (f32[2,36,8,128]{3,2,1,0:T(8,128)S(1)}, f32[2,36,8,128]{3,2,1,0:T(8,128)S(1)}, f32[2,36,8,128]{3,2,1,0:T(8,128)S(1)}, f32[2,36,8,128]{3,2,1,0:T(...) custom-call(s32[8]{0:T(128)S(1)} %copy-done, ...), custom_call_target="tpu_custom_call" | custom-call | flops 2000000000 | bytes 20000000 | tf_op jit(solution)/shard_map/wave_group/pallas_call | solution.py:372
  153.8 26.3 %collective-permute-start.10 = (f32[36,4,4096]{2,1,0:T(4,128)S(1)}, f32[36,4,4096]{2,1,0:T(4,128)S(1)}, u32[]{:S(2)}, u32[]{:S(2)}) collective-permute-start(f32[36,4,4096]{2,1,0:T(4,128)S(1)} %get-tuple-element.320), channel_id=1, source_target_pairs={{0,1},{1,2},{2,3},{4,5},{5,6},{6,7},{8,9},{9,10},{10,11},{12,13},{... | collective-permute-start | bytes 7077896 | tf_op jit(solution)/shard_map/ppermute | solution.py:541
  186.6 43.9 %wave_group.6 = (f32[2,36,8,128]{3,2,1,0:T(8,128)S(1)}, f32[2,36,8,128]{3,2,1,0:T(8,128)S(1)}, f32[2,36,8,128]{3,2,1,0:T(8,128)S(1)}, f32[2,36,8,128]{3,2,1,0:T(...) custom-call(s32[8]{0:T(128)S(1)} %copy-done, ...), custom_call_target="tpu_custom_call" | custom-call | flops 2000000000 | bytes 20000000 | tf_op jit(solution)/shard_map/wave_group/pallas_call | solution.py:372
  235.6 25.6 %collective-permute-start.12 = (f32[36,4,4096]{2,1,0:T(4,128)S(1)}, f32[36,4,4096]{2,1,0:T(4,128)S(1)}, u32[]{:S(2)}, u32[]{:S(2)}) collective-permute-start(f32[36,4,4096]{2,1,0:T(4,128)S(1)} %get-tuple-element.318), channel_id=1, source_target_pairs={{0,1},{1,2},{2,3},{4,5},{5,6},{6,7},{8,9},{9,10},{10,11},{12,13},{... | collective-permute-start | bytes 7077896 | tf_op jit(solution)/shard_map/ppermute | solution.py:541
  266.3 12.6 %collective-permute-done.13.rest_4_ = f32[4,36,8,128]{3,2,1,0:T(8,128)S(1)} collective-permute-done((f32[4,36,8,128]{3,2,1,0:T(8,128)S(1)}, f32[4,36,8,128]{3,2,1,0:T(8,128)S(1)}, u32[]{:S(2)}, u32[]{:S(2)}) %collective-permute-start.13) | collective-permute-done | bytes 589856 | tf_op jit(solution)/shard_map/ppermute | solution.py:577
  283.8 20.1 %collective-permute-done.21.rest_12_ = f32[4,36,8,128]{3,2,1,0:T(8,128)S(1)} collective-permute-done((f32[4,36,8,128]{3,2,1,0:T(8,128)S(1)}, f32[4,36,8,128]{3,2,1,0:T(8,128)S(1)}, u32[]{:S(2)}, u32[]{:S(2)}) %collective-permute-start.21) | collective-permute-done | bytes 589856 | tf_op jit(solution)/shard_map/ppermute | solution.py:577
  304.0 29.9 %collective-permute-done.25.rest_16_ = f32[4,36,8,128]{3,2,1,0:T(8,128)S(1)} collective-permute-done((f32[4,36,8,128]{3,2,1,0:T(8,128)S(1)}, f32[4,36,8,128]{3,2,1,0:T(8,128)S(1)}, u32[]{:S(2)}, u32[]{:S(2)}) %collective-permute-start.25) | collective-permute-done | bytes 589856 | tf_op jit(solution)/shard_map/ppermute | solution.py:577
  334.3 24.9 %collective-permute-done.29.rest_20_ = f32[4,36,8,128]{3,2,1,0:T(8,128)S(1)} collective-permute-done((f32[4,36,8,128]{3,2,1,0:T(8,128)S(1)}, f32[4,36,8,128]{3,2,1,0:T(8,128)S(1)}, u32[]{:S(2)}, u32[]{:S(2)}) %collective-permute-start.29) | collective-permute-done | bytes 589856 | tf_op jit(solution)/shard_map/ppermute | solution.py:577
  360.7 11.1 collective-permute-done.33.rest_24_
  371.8 12.8 %collective-permute-done.37.rest_28_ = f32[4,36,8,128]{3,2,1,0:T(8,128)S(1)} collective-permute-done((f32[4,36,8,128]{3,2,1,0:T(8,128)S(1)}, f32[4,36,8,128]{3,2,1,0:T(8,128)S(1)}, u32[]{:S(2)}, u32[]{:S(2)}) %collective-permute-start.37) | collective-permute-done | bytes 589856 | tf_op jit(solution)/shard_map/ppermute | solution.py:577
  398.0 17.0 %collective-permute-done.57.rest_17_ = f32[2,36,8,128]{3,2,1,0:T(8,128)S(1)} collective-permute-done((f32[2,36,8,128]{3,2,1,0:T(8,128)S(1)}, f32[2,36,8,128]{3,2,1,0:T(8,128)S(1)}, u32[]{:S(2)}, u32[]{:S(2)}) %collective-permute-start.57) | collective-permute-done | bytes 294944 | tf_op jit(solution)/shard_map/ppermute | solution.py:577
  415.4 12.2 collective-permute-done.60.rest_21_
  434.2 44.0 %wave_group.7 = (f32[2,36,8,128]{3,2,1,0:T(8,128)S(1)}, f32[2,36,8,128]{3,2,1,0:T(8,128)S(1)}, f32[2,36,8,128]{3,2,1,0:T(8,128)}, f32[2,36,8,128]{3,2,1,0:T(8,12...) custom-call(s32[8]{0:T(128)S(1)} %copy-done, ...), custom_call_target="tpu_custom_call" | custom-call | flops 2000000000 | bytes 20000000 | tf_op jit(solution)/shard_map/wave_group/pallas_call | solution.py:372
  490.4 24.2 %collective-permute-done.58.rest_18_ = f32[2,36,8,128]{3,2,1,0:T(8,128)} collective-permute-done((f32[2,36,8,128]{3,2,1,0:T(8,128)S(1)}, f32[2,36,8,128]{3,2,1,0:T(8,128)}, u32[]{:S(2)}, u32[]{:S(2)}) %collective-permute-start.58) | collective-permute-done | bytes 294944 | tf_op jit(solution)/shard_map/ppermute | solution.py:577
  544.2 9.0 collective-permute-done.20.rest_11_
  594.1 15.7 %collective-permute-done.28.rest_19_ = f32[2,36,8,128]{3,2,1,0:T(8,128)} collective-permute-done((f32[2,36,8,128]{3,2,1,0:T(8,128)}, f32[2,36,8,128]{3,2,1,0:T(8,128)}, u32[]{:S(2)}, u32[]{:S(2)}) %collective-permute-start.28) | collective-permute-done | bytes 294944 | tf_op jit(solution)/shard_map/ppermute | solution.py:577
  630.0 15.8 %collective-permute-start.65 = (f32[2,36,8,128]{3,2,1,0:T(8,128)}, f32[2,36,8,128]{3,2,1,0:T(8,128)S(1)}, u32[]{:S(2)}, u32[]{:S(2)}) collective-permute-start(f32[2,36,8,128]{3,2,1,0:T(8,128)} %copy-done.11), channel_id=1, source_target_pairs={{0,24},{4,28},{8,16},{12,20},{16,8},{20,12},{24,0},{28,4},{1,25},{... | collective-permute-start | bytes 884744 | tf_op jit(solution)/shard_map/ppermute | solution.py:577
  646.1 9.6 fusion
  660.5 22.0 %collective-permute-done.62.rest_23_ = f32[2,36,8,128]{3,2,1,0:T(8,128)S(1)} collective-permute-done((f32[2,36,8,128]{3,2,1,0:T(8,128)}, f32[2,36,8,128]{3,2,1,0:T(8,128)S(1)}, u32[]{:S(2)}, u32[]{:S(2)}) %collective-permute-start.62) | collective-permute-done | bytes 294944 | tf_op jit(solution)/shard_map/ppermute | solution.py:577
  682.5 16.2 %collective-permute-done.65.rest_27_ = f32[2,36,8,128]{3,2,1,0:T(8,128)S(1)} collective-permute-done((f32[2,36,8,128]{3,2,1,0:T(8,128)}, f32[2,36,8,128]{3,2,1,0:T(8,128)S(1)}, u32[]{:S(2)}, u32[]{:S(2)}) %collective-permute-start.65) | collective-permute-done | bytes 294944 | tf_op jit(solution)/shard_map/ppermute | solution.py:577
  709.3 54.9 %source_block.3 = (f32[2,144,8,128]{3,2,1,0:T(8,128)}, f32[2,144,8,128]{3,2,1,0:T(8,128)}, f32[2,144,8,128]{3,2,1,0:T(8,128)}, f32[2,144,8,128]{3,2,1,0:T(8,128)...) custom-call(bf16[2304,1152]{1,0:T(8,128)(2,1)} %get-tuple-element.32, ...), custom_call_target="tpu_custom_call" | custom-call | flops 4000000000 | bytes 40000000 | tf_op jit(solution)/shard_map/source_block/pallas_call | solution.py:465
  770.7 34.9 %collective-permute-done.39.rest_30_ = f32[2,36,8,128]{3,2,1,0:T(8,128)S(1)} collective-permute-done((f32[2,36,8,128]{3,2,1,0:T(8,128)S(1)}, f32[2,36,8,128]{3,2,1,0:T(8,128)S(1)}, u32[]{:S(2)}, u32[]{:S(2)}) %collective-permute-start.39) | collective-permute-done | bytes 294944 | tf_op jit(solution)/shard_map/ppermute | solution.py:577
  816.1 51.6 %collective-permute-start.73 = (f32[2,144,8,128]{3,2,1,0:T(8,128)}, f32[2,144,8,128]{3,2,1,0:T(8,128)}, u32[]{:S(2)}, u32[]{:S(2)}) collective-permute-start(f32[2,144,8,128]{3,2,1,0:T(8,128)} %get-tuple-element.313), channel_id=1, source_target_pairs={{0,20},{4,16},{8,28},{12,24},{16,4},{20,0},{24,12},{28,8},{1,21},{... | collective-permute-start | bytes 3538952 | tf_op jit(solution)/shard_map/ppermute | solution.py:616
  867.7 54.7 %source_block.2 = (f32[2,144,8,128]{3,2,1,0:T(8,128)}, f32[2,144,8,128]{3,2,1,0:T(8,128)}, f32[2,144,8,128]{3,2,1,0:T(8,128)}, f32[2,144,8,128]{3,2,1,0:T(8,128)...) custom-call(bf16[2304,1152]{1,0:T(8,128)(2,1)} %get-tuple-element.32, ...), custom_call_target="tpu_custom_call" | custom-call | flops 4000000000 | bytes 40000000 | tf_op jit(solution)/shard_map/source_block/pallas_call | solution.py:465
  936.7 57.9 %collective-permute-done.74.rest_6_ = f32[2,144,8,128]{3,2,1,0:T(8,128)} collective-permute-done((f32[2,144,8,128]{3,2,1,0:T(8,128)}, f32[2,144,8,128]{3,2,1,0:T(8,128)}, u32[]{:S(2)}, u32[]{:S(2)}) %collective-permute-start.74) | collective-permute-done | bytes 1179680 | tf_op jit(solution)/shard_map/ppermute | solution.py:616
  994.5 58.4 %collective-permute-done.75.rest_7_ = f32[2,144,8,128]{3,2,1,0:T(8,128)} collective-permute-done((f32[2,144,8,128]{3,2,1,0:T(8,128)}, f32[2,144,8,128]{3,2,1,0:T(8,128)}, u32[]{:S(2)}, u32[]{:S(2)}) %collective-permute-start.75) | collective-permute-done | bytes 1179680 | tf_op jit(solution)/shard_map/ppermute | solution.py:616
  1068.3 83.4 %collective-permute-done.44.rest_4_ = f32[2,144,8,128]{3,2,1,0:T(8,128)} collective-permute-done((f32[2,144,8,128]{3,2,1,0:T(8,128)}, f32[2,144,8,128]{3,2,1,0:T(8,128)}, u32[]{:S(2)}, u32[]{:S(2)}) %collective-permute-start.44) | collective-permute-done | bytes 1179680 | tf_op jit(solution)/shard_map/ppermute | solution.py:616
  1151.8 25.3 %collective-permute-done.45.rest_5_ = f32[2,144,8,128]{3,2,1,0:T(8,128)} collective-permute-done((f32[2,144,8,128]{3,2,1,0:T(8,128)}, f32[2,144,8,128]{3,2,1,0:T(8,128)}, u32[]{:S(2)}, u32[]{:S(2)}) %collective-permute-start.45) | collective-permute-done | bytes 1179680 | tf_op jit(solution)/shard_map/ppermute | solution.py:616
  1177.1 28.0 %collective-permute-done.46.rest_6_ = f32[2,144,8,128]{3,2,1,0:T(8,128)} collective-permute-done((f32[2,144,8,128]{3,2,1,0:T(8,128)}, f32[2,144,8,128]{3,2,1,0:T(8,128)}, u32[]{:S(2)}, u32[]{:S(2)}) %collective-permute-start.46) | collective-permute-done | bytes 1179680 | tf_op jit(solution)/shard_map/ppermute | solution.py:616
  1205.0 24.3 %collective-permute-done.47.rest_7_ = f32[2,144,8,128]{3,2,1,0:T(8,128)} collective-permute-done((f32[2,144,8,128]{3,2,1,0:T(8,128)}, f32[2,144,8,128]{3,2,1,0:T(8,128)}, u32[]{:S(2)}, u32[]{:S(2)}) %collective-permute-start.47) | collective-permute-done | bytes 1179680 | tf_op jit(solution)/shard_map/ppermute | solution.py:616
  (312 shorter events, 269.6 us)
Async XLA Ops:
  235.6 193.5 %collective-permute-start.12 = (f32[36,4,4096]{2,1,0:T(4,128)S(1)}, f32[36,4,4096]{2,1,0:T(4,128)S(1)}, u32[]{:S(2)}, u32[]{:S(2)}) collective-permute-start(f32[36,4,4096]{2,1,0:T(4,128)S(1)} %get-tuple-element.318), channel_id=1, source_target_pairs={{0,1},{1,2},{2,3},{4,5},{5,6},{6,7},{8,9},{9,10},{10,11},{12,13},{... | collective-permute-start | bytes 7077896 | tf_op jit(solution)/shard_map/ppermute | solution.py:541
  261.2 169.4 %collective-permute-start.11 = (f32[36,4,4096]{2,1,0:T(4,128)S(1)}, f32[36,4,4096]{2,1,0:T(4,128)S(1)}, u32[]{:S(2)}, u32[]{:S(2)}) collective-permute-start(f32[36,4,4096]{2,1,0:T(4,128)S(1)} %get-tuple-element.319), channel_id=1, source_target_pairs={{1,0},{2,1},{3,2},{5,4},{6,5},{7,6},{9,8},{10,9},{11,10},{13,12},{... | collective-permute-start | bytes 7077896 | tf_op jit(solution)/shard_map/ppermute | solution.py:540
  282.2 77.0 %collective-permute-start.29 = (f32[4,36,8,128]{3,2,1,0:T(8,128)S(1)}, f32[4,36,8,128]{3,2,1,0:T(8,128)S(1)}, u32[]{:S(2)}, u32[]{:S(2)}) collective-permute-start(f32[4,36,8,128]{3,2,1,0:T(8,128)S(1)} %get-tuple-element.272), channel_id=1, source_target_pairs={{0,20},{4,16},{8,28},{12,24},{16,4},{20,0},{24,12},{28,8},{1,21},{... | collective-permute-start | bytes 1769480 | tf_op jit(solution)/shard_map/ppermute | solution.py:577
  304.0 67.8 %collective-permute-start.33 = (f32[4,36,8,128]{3,2,1,0:T(8,128)S(1)}, f32[4,36,8,128]{3,2,1,0:T(8,128)S(1)}, u32[]{:S(2)}, u32[]{:S(2)}) collective-permute-start(f32[4,36,8,128]{3,2,1,0:T(8,128)S(1)} %get-tuple-element.276), channel_id=1, source_target_pairs={{0,24},{4,28},{8,16},{12,20},{16,8},{20,12},{24,0},{28,4},{1,25},{... | collective-permute-start | bytes 1769480 | tf_op jit(solution)/shard_map/ppermute | solution.py:577
  397.8 85.5 %collective-permute-start.63 = (f32[2,36,8,128]{3,2,1,0:T(8,128)S(1)}, f32[2,36,8,128]{3,2,1,0:T(8,128)S(1)}, u32[]{:S(2)}, u32[]{:S(2)}) collective-permute-start(f32[2,36,8,128]{3,2,1,0:T(8,128)S(1)} %get-tuple-element.304), channel_id=1, source_target_pairs={{0,24},{4,28},{8,16},{12,20},{16,8},{20,12},{24,0},{28,4},{1,25},{... | collective-permute-start | bytes 884744 | tf_op jit(solution)/shard_map/ppermute | solution.py:577
  415.0 71.1 %collective-permute-start.66 = (f32[2,36,8,128]{3,2,1,0:T(8,128)S(1)}, f32[2,36,8,128]{3,2,1,0:T(8,128)S(1)}, u32[]{:S(2)}, u32[]{:S(2)}) collective-permute-start(f32[2,36,8,128]{3,2,1,0:T(8,128)S(1)} %get-tuple-element.306), channel_id=1, source_target_pairs={{0,28},{4,24},{8,20},{12,16},{16,12},{20,8},{24,4},{28,0},{1,29},{... | collective-permute-start | bytes 884744 | tf_op jit(solution)/shard_map/ppermute | solution.py:577
  427.6 58.8 %collective-permute-start.49 = (f32[2,36,8,128]{3,2,1,0:T(8,128)S(1)}, f32[2,36,8,128]{3,2,1,0:T(8,128)S(1)}, u32[]{:S(2)}, u32[]{:S(2)}) collective-permute-start(f32[2,36,8,128]{3,2,1,0:T(8,128)S(1)} %get-tuple-element.295), channel_id=1, source_target_pairs={{0,4},{4,0},{8,12},{12,8},{16,20},{20,16},{24,28},{28,24},{1,5},{5... | collective-permute-start | bytes 884744 | tf_op jit(solution)/shard_map/ppermute | solution.py:577
  429.1 59.7 %collective-permute-start.52 = (f32[2,36,8,128]{3,2,1,0:T(8,128)S(1)}, f32[2,36,8,128]{3,2,1,0:T(8,128)}, u32[]{:S(2)}, u32[]{:S(2)}) collective-permute-start(f32[2,36,8,128]{3,2,1,0:T(8,128)S(1)} %get-tuple-element.297), channel_id=1, source_target_pairs={{0,8},{4,12},{8,0},{12,4},{16,24},{20,28},{24,16},{28,20},{1,9},{5... | collective-permute-start | bytes 884744 | tf_op jit(solution)/shard_map/ppermute | solution.py:577
  432.1 57.8 %collective-permute-start.55 = (f32[2,36,8,128]{3,2,1,0:T(8,128)S(1)}, f32[2,36,8,128]{3,2,1,0:T(8,128)}, u32[]{:S(2)}, u32[]{:S(2)}) collective-permute-start(f32[2,36,8,128]{3,2,1,0:T(8,128)S(1)} %get-tuple-element.299), channel_id=1, source_target_pairs={{0,12},{4,8},{8,4},{12,0},{16,28},{20,24},{24,20},{28,16},{1,13},{... | collective-permute-start | bytes 884744 | tf_op jit(solution)/shard_map/ppermute | solution.py:577
  565.8 64.1 %collective-permute-start.50 = (f32[2,36,8,128]{3,2,1,0:T(8,128)}, f32[2,36,8,128]{3,2,1,0:T(8,128)}, u32[]{:S(2)}, u32[]{:S(2)}) collective-permute-start(f32[2,36,8,128]{3,2,1,0:T(8,128)} %get-tuple-element.250), channel_id=1, source_target_pairs={{0,4},{4,0},{8,12},{12,8},{16,20},{20,16},{24,28},{28,24},{1,5},{5... | collective-permute-start | bytes 884744 | tf_op jit(solution)/shard_map/ppermute | solution.py:577
  572.2 73.6 %collective-permute-start.53 = (f32[2,36,8,128]{3,2,1,0:T(8,128)}, f32[2,36,8,128]{3,2,1,0:T(8,128)}, u32[]{:S(2)}, u32[]{:S(2)}) collective-permute-start(f32[2,36,8,128]{3,2,1,0:T(8,128)} %get-tuple-element.251), channel_id=1, source_target_pairs={{0,8},{4,12},{8,0},{12,4},{16,24},{20,28},{24,16},{28,20},{1,9},{5... | collective-permute-start | bytes 884744 | tf_op jit(solution)/shard_map/ppermute | solution.py:577
  630.0 68.8 %collective-permute-start.65 = (f32[2,36,8,128]{3,2,1,0:T(8,128)}, f32[2,36,8,128]{3,2,1,0:T(8,128)S(1)}, u32[]{:S(2)}, u32[]{:S(2)}) collective-permute-start(f32[2,36,8,128]{3,2,1,0:T(8,128)} %copy-done.11), channel_id=1, source_target_pairs={{0,24},{4,28},{8,16},{12,20},{16,8},{20,12},{24,0},{28,4},{1,25},{... | collective-permute-start | bytes 884744 | tf_op jit(solution)/shard_map/ppermute | solution.py:577
  645.8 59.5 %collective-permute-start.68 = (f32[2,36,8,128]{3,2,1,0:T(8,128)}, f32[2,36,8,128]{3,2,1,0:T(8,128)S(1)}, u32[]{:S(2)}, u32[]{:S(2)}) collective-permute-start(f32[2,36,8,128]{3,2,1,0:T(8,128)} %copy-done.10), channel_id=1, source_target_pairs={{0,28},{4,24},{8,20},{12,16},{16,12},{20,8},{24,4},{28,0},{1,29},{... | collective-permute-start | bytes 884744 | tf_op jit(solution)/shard_map/ppermute | solution.py:577
  655.7 108.5 %collective-permute-start.32 = (f32[2,36,8,128]{3,2,1,0:T(8,128)S(1)}, f32[2,36,8,128]{3,2,1,0:T(8,128)S(1)}, u32[]{:S(2)}, u32[]{:S(2)}) collective-permute-start(f32[2,36,8,128]{3,2,1,0:T(8,128)S(1)} %get-tuple-element.275), channel_id=1, source_target_pairs={{0,20},{4,16},{8,28},{12,24},{16,4},{20,0},{24,12},{28,8},{1,21},{... | collective-permute-start | bytes 884744 | tf_op jit(solution)/shard_map/ppermute | solution.py:577
  656.7 108.0 %collective-permute-start.34 = (f32[2,36,8,128]{3,2,1,0:T(8,128)S(1)}, f32[2,36,8,128]{3,2,1,0:T(8,128)S(1)}, u32[]{:S(2)}, u32[]{:S(2)}) collective-permute-start(f32[2,36,8,128]{3,2,1,0:T(8,128)S(1)} %get-tuple-element.277), channel_id=1, source_target_pairs={{0,24},{4,28},{8,16},{12,20},{16,8},{20,12},{24,0},{28,4},{1,25},{... | collective-permute-start | bytes 884744 | tf_op jit(solution)/shard_map/ppermute | solution.py:577
  682.5 82.2 %collective-permute-start.35 = (f32[2,36,8,128]{3,2,1,0:T(8,128)S(1)}, f32[2,36,8,128]{3,2,1,0:T(8,128)S(1)}, u32[]{:S(2)}, u32[]{:S(2)}) collective-permute-start(f32[2,36,8,128]{3,2,1,0:T(8,128)S(1)} %get-tuple-element.278), channel_id=1, source_target_pairs={{0,24},{4,28},{8,16},{12,20},{16,8},{20,12},{24,0},{28,4},{1,25},{... | collective-permute-start | bytes 884744 | tf_op jit(solution)/shard_map/ppermute | solution.py:577
  698.7 69.7 %collective-permute-start.36 = (f32[2,36,8,128]{3,2,1,0:T(8,128)S(1)}, f32[2,36,8,128]{3,2,1,0:T(8,128)S(1)}, u32[]{:S(2)}, u32[]{:S(2)}) collective-permute-start(f32[2,36,8,128]{3,2,1,0:T(8,128)S(1)} %get-tuple-element.279), channel_id=1, source_target_pairs={{0,24},{4,28},{8,16},{12,20},{16,8},{20,12},{24,0},{28,4},{1,25},{... | collective-permute-start | bytes 884744 | tf_op jit(solution)/shard_map/ppermute | solution.py:577
  705.3 63.9 %collective-permute-start.38 = (f32[2,36,8,128]{3,2,1,0:T(8,128)S(1)}, f32[2,36,8,128]{3,2,1,0:T(8,128)}, u32[]{:S(2)}, u32[]{:S(2)}) collective-permute-start(f32[2,36,8,128]{3,2,1,0:T(8,128)S(1)} %get-tuple-element.281), channel_id=1, source_target_pairs={{0,28},{4,24},{8,20},{12,16},{16,12},{20,8},{24,4},{28,0},{1,29},{... | collective-permute-start | bytes 884744 | tf_op jit(solution)/shard_map/ppermute | solution.py:577
  764.2 158.2 %collective-permute-start.69 = (f32[2,144,8,128]{3,2,1,0:T(8,128)}, f32[2,144,8,128]{3,2,1,0:T(8,128)S(1)}, u32[]{:S(2)}, u32[]{:S(2)}) collective-permute-start(f32[2,144,8,128]{3,2,1,0:T(8,128)} %get-tuple-element.309), channel_id=1, source_target_pairs={{0,4},{4,0},{8,12},{12,8},{16,20},{20,16},{24,28},{28,24},{1,5},{5... | collective-permute-start | bytes 3538952 | tf_op jit(solution)/shard_map/ppermute | solution.py:616
  764.7 161.1 %collective-permute-start.70 = (f32[2,144,8,128]{3,2,1,0:T(8,128)}, f32[2,144,8,128]{3,2,1,0:T(8,128)S(1)}, u32[]{:S(2)}, u32[]{:S(2)}) collective-permute-start(f32[2,144,8,128]{3,2,1,0:T(8,128)} %get-tuple-element.310), channel_id=1, source_target_pairs={{0,8},{4,12},{8,0},{12,4},{16,24},{20,28},{24,16},{28,20},{1,9},{5... | collective-permute-start | bytes 3538952 | tf_op jit(solution)/shard_map/ppermute | solution.py:616
  765.5 161.4 %collective-permute-start.71 = (f32[2,144,8,128]{3,2,1,0:T(8,128)}, f32[2,144,8,128]{3,2,1,0:T(8,128)S(1)}, u32[]{:S(2)}, u32[]{:S(2)}) collective-permute-start(f32[2,144,8,128]{3,2,1,0:T(8,128)} %get-tuple-element.311), channel_id=1, source_target_pairs={{0,12},{4,8},{8,4},{12,0},{16,28},{20,24},{24,20},{28,16},{1,13},{... | collective-permute-start | bytes 3538952 | tf_op jit(solution)/shard_map/ppermute | solution.py:616
  769.2 158.3 %collective-permute-start.72 = (f32[2,144,8,128]{3,2,1,0:T(8,128)}, f32[2,144,8,128]{3,2,1,0:T(8,128)S(1)}, u32[]{:S(2)}, u32[]{:S(2)}) collective-permute-start(f32[2,144,8,128]{3,2,1,0:T(8,128)} %get-tuple-element.312), channel_id=1, source_target_pairs={{0,16},{4,20},{8,24},{12,28},{16,0},{20,4},{24,8},{28,12},{1,17},{... | collective-permute-start | bytes 3538952 | tf_op jit(solution)/shard_map/ppermute | solution.py:616
  816.1 120.5 %collective-permute-start.73 = (f32[2,144,8,128]{3,2,1,0:T(8,128)}, f32[2,144,8,128]{3,2,1,0:T(8,128)}, u32[]{:S(2)}, u32[]{:S(2)}) collective-permute-start(f32[2,144,8,128]{3,2,1,0:T(8,128)} %get-tuple-element.313), channel_id=1, source_target_pairs={{0,20},{4,16},{8,28},{12,24},{16,4},{20,0},{24,12},{28,8},{1,21},{... | collective-permute-start | bytes 3538952 | tf_op jit(solution)/shard_map/ppermute | solution.py:616
  922.4 72.1 %collective-permute-start.74 = (f32[2,144,8,128]{3,2,1,0:T(8,128)}, f32[2,144,8,128]{3,2,1,0:T(8,128)}, u32[]{:S(2)}, u32[]{:S(2)}) collective-permute-start(f32[2,144,8,128]{3,2,1,0:T(8,128)} %get-tuple-element.314), channel_id=1, source_target_pairs={{0,24},{4,28},{8,16},{12,20},{16,8},{20,12},{24,0},{28,4},{1,25},{... | collective-permute-start | bytes 3538952 | tf_op jit(solution)/shard_map/ppermute | solution.py:616
  925.8 127.1 %collective-permute-start.75 = (f32[2,144,8,128]{3,2,1,0:T(8,128)}, f32[2,144,8,128]{3,2,1,0:T(8,128)}, u32[]{:S(2)}, u32[]{:S(2)}) collective-permute-start(f32[2,144,8,128]{3,2,1,0:T(8,128)} %get-tuple-element.315), channel_id=1, source_target_pairs={{0,28},{4,24},{8,20},{12,16},{16,12},{20,8},{24,4},{28,0},{1,29},{... | collective-permute-start | bytes 3538952 | tf_op jit(solution)/shard_map/ppermute | solution.py:616
  926.9 126.0 %collective-permute-start.41 = (f32[2,144,8,128]{3,2,1,0:T(8,128)}, f32[2,144,8,128]{3,2,1,0:T(8,128)S(1)}, u32[]{:S(2)}, u32[]{:S(2)}) collective-permute-start(f32[2,144,8,128]{3,2,1,0:T(8,128)} %get-tuple-element.285), channel_id=1, source_target_pairs={{0,4},{4,0},{8,12},{12,8},{16,20},{20,16},{24,28},{28,24},{1,5},{5... | collective-permute-start | bytes 3538952 | tf_op jit(solution)/shard_map/ppermute | solution.py:616
  928.5 124.5 %collective-permute-start.42 = (f32[2,144,8,128]{3,2,1,0:T(8,128)}, f32[2,144,8,128]{3,2,1,0:T(8,128)S(1)}, u32[]{:S(2)}, u32[]{:S(2)}) collective-permute-start(f32[2,144,8,128]{3,2,1,0:T(8,128)} %get-tuple-element.286), channel_id=1, source_target_pairs={{0,8},{4,12},{8,0},{12,4},{16,24},{20,28},{24,16},{28,20},{1,9},{5... | collective-permute-start | bytes 3538952 | tf_op jit(solution)/shard_map/ppermute | solution.py:616
  936.6 131.8 %collective-permute-start.43 = (f32[2,144,8,128]{3,2,1,0:T(8,128)}, f32[2,144,8,128]{3,2,1,0:T(8,128)}, u32[]{:S(2)}, u32[]{:S(2)}) collective-permute-start(f32[2,144,8,128]{3,2,1,0:T(8,128)} %get-tuple-element.287), channel_id=1, source_target_pairs={{0,12},{4,8},{8,4},{12,0},{16,28},{20,24},{24,20},{28,16},{1,13},{... | collective-permute-start | bytes 3538952 | tf_op jit(solution)/shard_map/ppermute | solution.py:616
  994.5 157.3 %collective-permute-start.44 = (f32[2,144,8,128]{3,2,1,0:T(8,128)}, f32[2,144,8,128]{3,2,1,0:T(8,128)}, u32[]{:S(2)}, u32[]{:S(2)}) collective-permute-start(f32[2,144,8,128]{3,2,1,0:T(8,128)} %get-tuple-element.288), channel_id=1, source_target_pairs={{0,16},{4,20},{8,24},{12,28},{16,0},{20,4},{24,8},{28,12},{1,17},{... | collective-permute-start | bytes 3538952 | tf_op jit(solution)/shard_map/ppermute | solution.py:616
  1052.9 124.1 %collective-permute-start.45 = (f32[2,144,8,128]{3,2,1,0:T(8,128)}, f32[2,144,8,128]{3,2,1,0:T(8,128)}, u32[]{:S(2)}, u32[]{:S(2)}) collective-permute-start(f32[2,144,8,128]{3,2,1,0:T(8,128)} %get-tuple-element.289), channel_id=1, source_target_pairs={{0,20},{4,16},{8,28},{12,24},{16,4},{20,0},{24,12},{28,8},{1,21},{... | collective-permute-start | bytes 3538952 | tf_op jit(solution)/shard_map/ppermute | solution.py:616
  1052.9 152.1 %collective-permute-start.46 = (f32[2,144,8,128]{3,2,1,0:T(8,128)}, f32[2,144,8,128]{3,2,1,0:T(8,128)}, u32[]{:S(2)}, u32[]{:S(2)}) collective-permute-start(f32[2,144,8,128]{3,2,1,0:T(8,128)} %get-tuple-element.290), channel_id=1, source_target_pairs={{0,24},{4,28},{8,16},{12,20},{16,8},{20,12},{24,0},{28,4},{1,25},{... | collective-permute-start | bytes 3538952 | tf_op jit(solution)/shard_map/ppermute | solution.py:616
  1053.1 176.3 %collective-permute-start.47 = (f32[2,144,8,128]{3,2,1,0:T(8,128)}, f32[2,144,8,128]{3,2,1,0:T(8,128)}, u32[]{:S(2)}, u32[]{:S(2)}) collective-permute-start(f32[2,144,8,128]{3,2,1,0:T(8,128)} %get-tuple-element.291), channel_id=1, source_target_pairs={{0,28},{4,24},{8,20},{12,16},{16,12},{20,8},{24,4},{28,0},{1,29},{... | collective-permute-start | bytes 3538952 | tf_op jit(solution)/shard_map/ppermute | solution.py:616
  (114 other events, 3932.2 us)

commit v2 on v1

--- a/solution.py
+++ b/solution.py
@@ -227,7 +227,7 @@
 
 SUBLANES = 8
 LANES = 128
-HALVES = 2
+BLOCKS = 4
 
 
 def partner_routes(count, step):
@@ -245,7 +245,7 @@
     count = gathered_ref.shape[0]
     tile_width = width // count
     per_tile = tile_width // LANES
-    per_part = per_tile // parts
+    begins = [sum(parts[:n]) for n in range(len(parts))]
     me = lax.axis_index("comp")
     frequency = me * groups + group
     loads = [pltpu.make_async_copy(spec_ref.at[pl.ds(group * dirs, dirs)], own_a, in_sems.at[0])]
@@ -346,10 +346,10 @@
     stores = []
     for k in range(count):
         tile = order_ref[me ^ k]
-        for part in range(parts):
-            n = k * parts + part
+        for part, size in enumerate(parts):
+            n = k * len(parts) + part
             stores.append(
-                pltpu.make_async_copy(stage.at[tile, pl.ds(part * per_part, per_part)], outs[n], out_sems.at[n])
+                pltpu.make_async_copy(stage.at[tile, pl.ds(begins[part], size)], outs[n], out_sems.at[n])
             )
     for store in stores:
         store.start()
@@ -363,15 +363,15 @@
     _, rows, width = spectrum.shape
     count = gathered.shape[0]
     per_tile = width // count // LANES
-    pieces = count * parts
-    piece = jax.ShapeDtypeStruct((per_tile // parts, DIRS, rows, LANES), jnp.float32)
+    pieces = count * len(parts)
+    shapes = [jax.ShapeDtypeStruct((size, DIRS, rows, LANES), jnp.float32) for size in parts] * count
     smem = pl.BlockSpec(memory_space=pltpu.SMEM)
     hbm = pl.BlockSpec(memory_space=pltpu.HBM)
     vmem = pl.BlockSpec(memory_space=pltpu.VMEM)
     state = pltpu.VMEM((DIRS, rows, width), jnp.float32)
     return pl.pallas_call(
         functools.partial(wave_kernel, group=group, groups=groups, pieces=pieces, parts=parts),
-        out_shape=[piece] * pieces,
+        out_shape=shapes,
         in_specs=[smem, smem, smem, smem, hbm, hbm, vmem, vmem, vmem, vmem],
         out_specs=[hbm] * pieces,
         scratch_shapes=[
@@ -485,12 +485,12 @@
     return outs, drift
 
 
-def place_kernel(order_ref, *rest, count, half, seeded):
+def place_kernel(order_ref, *rest, first, count, half, seeded):
     ins = rest[:count]
     out_ref, stage, in_sems, out_sems = rest[count + seeded :]
     lane_tiles = ins[0].shape[0]
     me = lax.axis_index("comp")
-    tile_width = out_ref.shape[2] // count
+    tile_width = out_ref.shape[2] // order_ref.shape[0]
     loads = [pltpu.make_async_copy(ins[k], stage.at[k], in_sems.at[k]) for k in range(count)]
     for load in loads:
         load.start()
@@ -498,7 +498,7 @@
     for k in range(count):
         loads[k].wait()
         for tile in range(lane_tiles):
-            start = order_ref[me ^ k] * tile_width + (half * lane_tiles + tile) * LANES
+            start = order_ref[me ^ (first + k)] * tile_width + (half * lane_tiles + tile) * LANES
             stores.append(
                 pltpu.make_async_copy(
                     stage.at[k, tile],
@@ -511,13 +511,14 @@
         store.wait()
 
 
-def place_half(owner_map, pieces, target, half, width):
+def place_part(owner_map, pieces, target, half, width, ks):
     lane_tiles, per_device, rows, _ = pieces[0].shape
+    pieces = [pieces[k] for k in ks]
     count = len(pieces)
     seeded = int(target is not None)
     hbm = pl.BlockSpec(memory_space=pltpu.HBM)
     return pl.pallas_call(
-        functools.partial(place_kernel, count=count, half=half, seeded=seeded),
+        functools.partial(place_kernel, first=ks[0], count=count, half=half, seeded=seeded),
         out_shape=jax.ShapeDtypeStruct((per_device, rows, width), jnp.float32),
         in_specs=[pl.BlockSpec(memory_space=pltpu.SMEM)] + [hbm] * (count + seeded),
         out_specs=hbm,
@@ -527,7 +528,7 @@
             pltpu.SemaphoreType.DMA((count * lane_tiles,)),
         ],
         input_output_aliases={1 + count: 0} if seeded else {},
-        name="place_half",
+        name="place_part",
     )(owner_map, *pieces, *([target] if seeded else []))
 
 
@@ -578,45 +579,51 @@
 
     source = spectrum
     for g in range(groups):
-        parts = parts_of(g)
+        parts = parts_of(g, groups, tile_width // LANES)
         pieces = wave_group(
             owner_map, group_courant, refraction, angles, spectrum, gathered, *halo, ocean16, class16, g, groups, parts
         )
         interp, source, pieces = lax.optimization_barrier((interp, source, pieces))
+        if g == 0:
+            stacked_interp = jnp.concatenate([interp, interp.T], axis=0)
+            rounded = lax.reduce_precision(stacked_interp, 8, 7)
+            high = rounded.astype(jnp.bfloat16)
+            low = (stacked_interp - rounded).astype(jnp.bfloat16)
+            class16, high, low = lax.optimization_barrier((class16, high, low))
         if g < groups - 1:
             halo = band_rows(source[(g + 1) * DIRS : (g + 2) * DIRS], 1)
-        for part in range(parts):
+        for part in range(len(parts)):
             received[0, g, part] = pieces[part]
         for k in steps:
-            send(g, 0, k, pieces[k * parts])
-            for part in range(1, parts):
-                waiting[g, part, k] = pieces[k * parts + part]
-    waiting, pieces = lax.optimization_barrier((waiting, pieces))
+            send(g, 0, k, pieces[k * len(parts)])
+            for part in range(1, len(parts)):
+                waiting[g, part, k] = pieces[k * len(parts) + part]
+    waiting, received = lax.optimization_barrier((waiting, received))
     for (g, part, k), piece in waiting.items():
         send(g, part, k, piece)
-    stacked_interp = jnp.concatenate([interp, interp.T], axis=0)
-    rounded = lax.reduce_precision(stacked_interp, 8, 7)
-    high = rounded.astype(jnp.bfloat16)
-    low = (stacked_interp - rounded).astype(jnp.bfloat16)
     weights = jnp.broadcast_to(stokes_weights(interp.shape[0])[:, :, None], (2, interp.shape[0], LANES))
-    lane_tiles = tile_width // LANES // HALVES
+    lane_tiles = tile_width // LANES // BLOCKS
     spectrum_out = None
     drifts = []
     returned = []
-    for half in range(HALVES):
+    for half in range(BLOCKS):
         blocks, offsets = [], []
         for k in range(count):
             for g in range(groups):
                 split = (k, g, 1) in received
-                blocks.append(received[k, g, half if split else 0])
-                offsets.append(0 if split else half * lane_tiles)
+                part = int(split and half > 0)
+                blocks.append(received[k, g, part])
+                offsets.append((half - part) * lane_tiles)
         outs, drift = source_block(high, low, weights, blocks, offsets, lane_tiles, groups, count)
         drifts.append(drift)
-        returned.append(
-            [outs[0]] + [lax.ppermute(outs[k], "comp", partner_routes(count, k)) for k in steps]
-        )
-    for half in range(HALVES):
-        spectrum_out = place_half(owner_map, returned[half], spectrum_out, half, width)
+        back = [outs[0]]
+        for k in steps:
+            back.append(lax.ppermute(outs[k], "comp", partner_routes(count, k)))
+        returned.append(back)
+    for half in range(BLOCKS):
+        cuts = [0, count] if half < BLOCKS - 1 else [0, count // 2, count]
+        for ks in map(range, cuts[:-1], cuts[1:]):
+            spectrum_out = place_part(owner_map, returned[half], spectrum_out, half, width, ks)
     stokes = jnp.concatenate(drifts, axis=1).transpose(0, 2, 1, 3).reshape(2, rows, tile_width)
     tile_index = owner_map[comp_pos]
     order = owner_map[comp_pos ^ jnp.arange(count, dtype=jnp.int32)]
@@ -659,8 +666,9 @@
     return (spectrum_out, jnp.stack([east_new, north_new]))
 
 
-def parts_of(group):
-    return 1 if group == 0 else HALVES
+def parts_of(group, groups, lane_tiles):
+    size = lane_tiles // BLOCKS
+    return [size, lane_tiles - size] if group == groups - 1 else [lane_tiles]
 
 
 def fits(mesh, spectrum):
@@ -670,7 +678,7 @@
         (comps // count) % DIRS == 0
         and count & (count - 1) == 0
         and rows_all // mesh.shape["band"] == SUBLANES
-        and width % (count * HALVES * LANES) == 0
+        and width % (count * BLOCKS * LANES) == 0
     )
 
 

time: 1250 us -> 1060 us (0.85)
  the two profiles are of different devices: /device:TPU:8 before, /device:TPU:0 now
where the time goes in v2:
time: 1060 us; the launch traced here: 1040 us
  starting transfers between devices  380 us (36%)
  Pallas kernels  324 us (31%)
  waiting for transfers between devices  272 us (26%)
  local copies, waits for them, and re-layouts  47 us (4%)
  other arithmetic  13.7 us (1%)
    pallas_call x4, Pallas kernels, wave_group(): pl.pallas_call(functools.partial(wave_kernel, group=group, groups=groups,...  179 us
    ppermute x28, starting transfers between devices, local_fused(): back.append(lax.ppermute(outs[k], 'comp', partner_routes(count, k)))  174 us
    ppermute x35, starting transfers between devices, send(): received[k, g, part] = lax.ppermute(piece, 'comp', partner_routes(count, k))  134 us
    ppermute x35, waiting for transfers between devices, send(): received[k, g, part] = lax.ppermute(piece, 'comp', partner_routes(count, k))  132 us
    pallas_call x4, Pallas kernels, source_block(): pl.pallas_call(functools.partial(source_kernel, groups=groups, count=coun...  124 us
    ppermute x28, waiting for transfers between devices, local_fused(): back.append(lax.ppermute(outs[k], 'comp', partner_routes(count, k)))  121 us
    ppermute x5, starting transfers between devices, band_rows(): south = lax.ppermute(last, 'band', up)  59.3 us
    slice x4, local copies, waits for them, and re-layouts, band_rows(): last = lax.slice_in_dim(value, length - SUBSTEPS, length, axis=dim)  25 us
  transfers between devices with their start and end apart: 76, of which 17 were waited for; matrix products, arithmetic and copies ran while one was open for 4% of the time, Pallas kernels for 22%

profile of v2, /device:TPU:0, one launch (start us, length us, event | category | flops | bytes accessed | tf_op | source)
XLA Modules:
  0.0 1040.8 jit_solution(8721787481078753378)
XLA Ops:
  49.0 44.2 %wave_group.4 = (f32[4,36,8,128]{3,2,1,0:T(8,128)S(1)}, f32[4,36,8,128]{3,2,1,0:T(8,128)S(1)}, f32[4,36,8,128]{3,2,1,0:T(8,128)S(1)}, f32[4,36,8,128]{3,2,1,0:T(...) custom-call(s32[8]{0:T(128)S(1)} %copy-done, ...), custom_call_target="tpu_custom_call" | custom-call | flops 2000000000 | bytes 20000000 | tf_op jit(solution)/shard_map/wave_group/pallas_call | solution.py:372
  121.8 44.2 %wave_group.5 = (f32[4,36,8,128]{3,2,1,0:T(8,128)S(1)}, f32[4,36,8,128]{3,2,1,0:T(8,128)S(1)}, f32[4,36,8,128]{3,2,1,0:T(8,128)S(1)}, f32[4,36,8,128]{3,2,1,0:T(...) custom-call(s32[8]{0:T(128)S(1)} %copy-done, ...), custom_call_target="tpu_custom_call" | custom-call | flops 2000000000 | bytes 20000000 | tf_op jit(solution)/shard_map/wave_group/pallas_call | solution.py:372
  171.1 14.4 %collective-permute-start.10 = (f32[36,4,4096]{2,1,0:T(4,128)S(1)}, f32[36,4,4096]{2,1,0:T(4,128)S(1)}, u32[]{:S(2)}, u32[]{:S(2)}) collective-permute-start(f32[36,4,4096]{2,1,0:T(4,128)S(1)} %get-tuple-element.330), channel_id=1, source_target_pairs={{0,1},{1,2},{2,3},{4,5},{5,6},{6,7},{8,9},{9,10},{10,11},{12,13},{... | collective-permute-start | bytes 7077896 | tf_op jit(solution)/shard_map/ppermute | solution.py:542
  196.2 44.1 %wave_group.6 = (f32[4,36,8,128]{3,2,1,0:T(8,128)S(1)}, f32[4,36,8,128]{3,2,1,0:T(8,128)S(1)}, f32[4,36,8,128]{3,2,1,0:T(8,128)S(1)}, f32[4,36,8,128]{3,2,1,0:T(...) custom-call(s32[8]{0:T(128)S(1)} %copy-done, ...), custom_call_target="tpu_custom_call" | custom-call | flops 2000000000 | bytes 20000000 | tf_op jit(solution)/shard_map/wave_group/pallas_call | solution.py:372
  249.2 34.1 %collective-permute-start.12 = (f32[36,4,4096]{2,1,0:T(4,128)S(1)}, f32[36,4,4096]{2,1,0:T(4,128)S(1)}, u32[]{:S(2)}, u32[]{:S(2)}) collective-permute-start(f32[36,4,4096]{2,1,0:T(4,128)S(1)} %get-tuple-element.328), channel_id=1, source_target_pairs={{0,1},{1,2},{2,3},{4,5},{5,6},{6,7},{8,9},{9,10},{10,11},{12,13},{... | collective-permute-start | bytes 7077896 | tf_op jit(solution)/shard_map/ppermute | solution.py:542
  302.1 22.0 %collective-permute-start.26 = (f32[4,36,8,128]{3,2,1,0:T(8,128)S(1)}, f32[4,36,8,128]{3,2,1,0:T(8,128)S(1)}, u32[]{:S(2)}, u32[]{:S(2)}) collective-permute-start(f32[4,36,8,128]{3,2,1,0:T(8,128)S(1)} %get-tuple-element.237), channel_id=1, source_target_pairs={{0,16},{4,20},{8,24},{12,28},{16,0},{20,4},{24,8},{28,12},{1,17},{... | collective-permute-start | bytes 1769480 | tf_op jit(solution)/shard_map/ppermute | solution.py:578
  326.6 49.7 %collective-permute-done.26.rest_17_ = f32[4,36,8,128]{3,2,1,0:T(8,128)S(1)} collective-permute-done((f32[4,36,8,128]{3,2,1,0:T(8,128)S(1)}, f32[4,36,8,128]{3,2,1,0:T(8,128)S(1)}, u32[]{:S(2)}, u32[]{:S(2)}) %collective-permute-start.26) | collective-permute-done | bytes 589856 | tf_op jit(solution)/shard_map/ppermute | solution.py:578
  378.1 24.3 %collective-permute-done.30.rest_21_ = f32[4,36,8,128]{3,2,1,0:T(8,128)S(1)} collective-permute-done((f32[4,36,8,128]{3,2,1,0:T(8,128)S(1)}, f32[4,36,8,128]{3,2,1,0:T(8,128)S(1)}, u32[]{:S(2)}, u32[]{:S(2)}) %collective-permute-start.30) | collective-permute-done | bytes 589856 | tf_op jit(solution)/shard_map/ppermute | solution.py:578
  403.0 11.7 %collective-permute-start.19 = (f32[4,36,8,128]{3,2,1,0:T(8,128)S(1)}, f32[4,36,8,128]{3,2,1,0:T(8,128)S(1)}, u32[]{:S(2)}, u32[]{:S(2)}) collective-permute-start(f32[4,36,8,128]{3,2,1,0:T(8,128)S(1)} %get-tuple-element.230), channel_id=1, source_target_pairs={{0,8},{4,12},{8,0},{12,4},{16,24},{20,28},{24,16},{28,20},{1,9},{5... | collective-permute-start | bytes 1769480 | tf_op jit(solution)/shard_map/ppermute | solution.py:578
  414.7 13.1 %collective-permute-start.23 = (f32[4,36,8,128]{3,2,1,0:T(8,128)S(1)}, f32[4,36,8,128]{3,2,1,0:T(8,128)S(1)}, u32[]{:S(2)}, u32[]{:S(2)}) collective-permute-start(f32[4,36,8,128]{3,2,1,0:T(8,128)S(1)} %get-tuple-element.234), channel_id=1, source_target_pairs={{0,12},{4,8},{8,4},{12,0},{16,28},{20,24},{24,20},{28,16},{1,13},{... | collective-permute-start | bytes 1769480 | tf_op jit(solution)/shard_map/ppermute | solution.py:578
  436.9 47.0 %wave_group.7 = (f32[1,36,8,128]{3,2,1,0:T(8,128)S(1)}, f32[3,36,8,128]{3,2,1,0:T(8,128)S(1)}, f32[1,36,8,128]{3,2,1,0:T(8,128)S(1)}, f32[3,36,8,128]{3,2,1,0:T(...) custom-call(s32[8]{0:T(128)S(1)} %copy-done, ...), custom_call_target="tpu_custom_call" | custom-call | flops 2000000000 | bytes 20000000 | tf_op jit(solution)/shard_map/wave_group/pallas_call | solution.py:372
  495.6 13.4 %collective-permute-done.31.rest_22_ = f32[4,36,8,128]{3,2,1,0:T(8,128)S(1)} collective-permute-done((f32[4,36,8,128]{3,2,1,0:T(8,128)S(1)}, f32[4,36,8,128]{3,2,1,0:T(8,128)S(1)}, u32[]{:S(2)}, u32[]{:S(2)}) %collective-permute-start.31) | collective-permute-done | bytes 589856 | tf_op jit(solution)/shard_map/ppermute | solution.py:578
  509.0 12.6 %collective-permute-start.28 = (f32[1,36,8,128]{3,2,1,0:T(8,128)S(1)}, f32[1,36,8,128]{3,2,1,0:T(8,128)S(1)}, u32[]{:S(2)}, u32[]{:S(2)}) collective-permute-start(f32[1,36,8,128]{3,2,1,0:T(8,128)S(1)} %get-tuple-element.239), channel_id=1, source_target_pairs={{0,16},{4,20},{8,24},{12,28},{16,0},{20,4},{24,8},{28,12},{1,17},{... | collective-permute-start | bytes 442376 | tf_op jit(solution)/shard_map/ppermute | solution.py:578
  521.6 16.7 %collective-permute-start.32 = (f32[1,36,8,128]{3,2,1,0:T(8,128)S(1)}, f32[1,36,8,128]{3,2,1,0:T(8,128)S(1)}, u32[]{:S(2)}, u32[]{:S(2)}) collective-permute-start(f32[1,36,8,128]{3,2,1,0:T(8,128)S(1)} %get-tuple-element.243), channel_id=1, source_target_pairs={{0,20},{4,16},{8,28},{12,24},{16,4},{20,0},{24,12},{28,8},{1,21},{... | collective-permute-start | bytes 442376 | tf_op jit(solution)/shard_map/ppermute | solution.py:578
  565.6 21.6 %collective-permute-done.42.rest_11_ = f32[3,36,8,128]{3,2,1,0:T(8,128)S(1)} collective-permute-done((f32[3,36,8,128]{3,2,1,0:T(8,128)S(1)}, f32[3,36,8,128]{3,2,1,0:T(8,128)S(1)}, u32[]{:S(2)}, u32[]{:S(2)}) %collective-permute-start.42) | collective-permute-done | bytes 442400 | tf_op jit(solution)/shard_map/ppermute | solution.py:578
  591.2 30.9 %source_block.7 = (f32[1,144,8,128]{3,2,1,0:T(8,128)}, f32[1,144,8,128]{3,2,1,0:T(8,128)}, f32[1,144,8,128]{3,2,1,0:T(8,128)}, f32[1,144,8,128]{3,2,1,0:T(8,128)...) custom-call(bf16[2304,1152]{1,0:T(8,128)(2,1)} %get-tuple-element.17, ...), custom_call_target="tpu_custom_call" | custom-call | flops 4000000000 | bytes 40000000 | tf_op jit(solution)/shard_map/source_block/pallas_call | solution.py:465
  632.3 14.4 %collective-permute-start.73 = (f32[1,144,8,128]{3,2,1,0:T(8,128)}, f32[1,144,8,128]{3,2,1,0:T(8,128)}, u32[]{:S(2)}, u32[]{:S(2)}) collective-permute-start(f32[1,144,8,128]{3,2,1,0:T(8,128)} %get-tuple-element.321), channel_id=1, source_target_pairs={{0,20},{4,16},{8,28},{12,24},{16,4},{20,0},{24,12},{28,8},{1,21},{... | collective-permute-start | bytes 1769480 | tf_op jit(solution)/shard_map/ppermute | solution.py:621
  646.8 30.9 %source_block.6 = (f32[1,144,8,128]{3,2,1,0:T(8,128)}, f32[1,144,8,128]{3,2,1,0:T(8,128)}, f32[1,144,8,128]{3,2,1,0:T(8,128)}, f32[1,144,8,128]{3,2,1,0:T(8,128)...) custom-call(bf16[2304,1152]{1,0:T(8,128)(2,1)} %get-tuple-element.17, ...), custom_call_target="tpu_custom_call" | custom-call | flops 4000000000 | bytes 40000000 | tf_op jit(solution)/shard_map/source_block/pallas_call | solution.py:465
  686.4 20.5 %collective-permute-done.72.rest_4_ = f32[1,144,8,128]{3,2,1,0:T(8,128)} collective-permute-done((f32[1,144,8,128]{3,2,1,0:T(8,128)}, f32[1,144,8,128]{3,2,1,0:T(8,128)}, u32[]{:S(2)}, u32[]{:S(2)}) %collective-permute-start.72) | collective-permute-done | bytes 589856 | tf_op jit(solution)/shard_map/ppermute | solution.py:621
  706.9 12.7 %collective-permute-done.73.rest_5_ = f32[1,144,8,128]{3,2,1,0:T(8,128)} collective-permute-done((f32[1,144,8,128]{3,2,1,0:T(8,128)}, f32[1,144,8,128]{3,2,1,0:T(8,128)}, u32[]{:S(2)}, u32[]{:S(2)}) %collective-permute-start.73) | collective-permute-done | bytes 589856 | tf_op jit(solution)/shard_map/ppermute | solution.py:621
  719.6 20.2 %collective-permute-start.65 = (f32[1,144,8,128]{3,2,1,0:T(8,128)}, f32[1,144,8,128]{3,2,1,0:T(8,128)}, u32[]{:S(2)}, u32[]{:S(2)}) collective-permute-start(f32[1,144,8,128]{3,2,1,0:T(8,128)} %get-tuple-element.304), channel_id=1, source_target_pairs={{0,16},{4,20},{8,24},{12,28},{16,0},{20,4},{24,8},{28,12},{1,17},{... | collective-permute-start | bytes 1769480 | tf_op jit(solution)/shard_map/ppermute | solution.py:621
  739.8 19.9 %collective-permute-start.66 = (f32[1,144,8,128]{3,2,1,0:T(8,128)}, f32[1,144,8,128]{3,2,1,0:T(8,128)}, u32[]{:S(2)}, u32[]{:S(2)}) collective-permute-start(f32[1,144,8,128]{3,2,1,0:T(8,128)} %get-tuple-element.305), channel_id=1, source_target_pairs={{0,20},{4,16},{8,28},{12,24},{16,4},{20,0},{24,12},{28,8},{1,21},{... | collective-permute-start | bytes 1769480 | tf_op jit(solution)/shard_map/ppermute | solution.py:621
  762.9 31.0 %source_block.5 = (f32[1,144,8,128]{3,2,1,0:T(8,128)}, f32[1,144,8,128]{3,2,1,0:T(8,128)}, f32[1,144,8,128]{3,2,1,0:T(8,128)}, f32[1,144,8,128]{3,2,1,0:T(8,128)...) custom-call(bf16[2304,1152]{1,0:T(8,128)(2,1)} %get-tuple-element.17, ...), custom_call_target="tpu_custom_call" | custom-call | flops 4000000000 | bytes 40000000 | tf_op jit(solution)/shard_map/source_block/pallas_call | solution.py:465
  803.8 17.0 %collective-permute-done.66.rest_5_ = f32[1,144,8,128]{3,2,1,0:T(8,128)} collective-permute-done((f32[1,144,8,128]{3,2,1,0:T(8,128)}, f32[1,144,8,128]{3,2,1,0:T(8,128)}, u32[]{:S(2)}, u32[]{:S(2)}) %collective-permute-start.66) | collective-permute-done | bytes 589856 | tf_op jit(solution)/shard_map/ppermute | solution.py:621
  820.8 20.3 %collective-permute-start.58 = (f32[1,144,8,128]{3,2,1,0:T(8,128)}, f32[1,144,8,128]{3,2,1,0:T(8,128)}, u32[]{:S(2)}, u32[]{:S(2)}) collective-permute-start(f32[1,144,8,128]{3,2,1,0:T(8,128)} %get-tuple-element.296), channel_id=1, source_target_pairs={{0,16},{4,20},{8,24},{12,28},{16,0},{20,4},{24,8},{28,12},{1,17},{... | collective-permute-start | bytes 1769480 | tf_op jit(solution)/shard_map/ppermute | solution.py:621
  841.1 31.0 %source_block.4 = (f32[1,144,8,128]{3,2,1,0:T(8,128)}, f32[1,144,8,128]{3,2,1,0:T(8,128)}, f32[1,144,8,128]{3,2,1,0:T(8,128)}, f32[1,144,8,128]{3,2,1,0:T(8,128)...) custom-call(bf16[2304,1152]{1,0:T(8,128)(2,1)} %get-tuple-element.17, ...), custom_call_target="tpu_custom_call" | custom-call | flops 4000000000 | bytes 40000000 | tf_op jit(solution)/shard_map/source_block/pallas_call | solution.py:465
  877.6 31.6 %collective-permute-done.58.rest_4_ = f32[1,144,8,128]{3,2,1,0:T(8,128)} collective-permute-done((f32[1,144,8,128]{3,2,1,0:T(8,128)}, f32[1,144,8,128]{3,2,1,0:T(8,128)}, u32[]{:S(2)}, u32[]{:S(2)}) %collective-permute-start.58) | collective-permute-done | bytes 589856 | tf_op jit(solution)/shard_map/ppermute | solution.py:621
  910.1 18.1 %collective-permute-done.59.rest_5_ = f32[1,144,8,128]{3,2,1,0:T(8,128)} collective-permute-done((f32[1,144,8,128]{3,2,1,0:T(8,128)}, f32[1,144,8,128]{3,2,1,0:T(8,128)}, u32[]{:S(2)}, u32[]{:S(2)}) %collective-permute-start.59) | collective-permute-done | bytes 589856 | tf_op jit(solution)/shard_map/ppermute | solution.py:621
  928.2 20.3 %collective-permute-start.49 = (f32[1,144,8,128]{3,2,1,0:T(8,128)}, f32[1,144,8,128]{3,2,1,0:T(8,128)}, u32[]{:S(2)}, u32[]{:S(2)}) collective-permute-start(f32[1,144,8,128]{3,2,1,0:T(8,128)} %get-tuple-element.285), channel_id=1, source_target_pairs={{0,20},{4,16},{8,28},{12,24},{16,4},{20,0},{24,12},{28,8},{1,21},{... | collective-permute-start | bytes 1769480 | tf_op jit(solution)/shard_map/ppermute | solution.py:621
  950.1 34.7 %collective-permute-start.51 = (f32[1,144,8,128]{3,2,1,0:T(8,128)}, f32[1,144,8,128]{3,2,1,0:T(8,128)}, u32[]{:S(2)}, u32[]{:S(2)}) collective-permute-start(f32[1,144,8,128]{3,2,1,0:T(8,128)} %get-tuple-element.287), channel_id=1, source_target_pairs={{0,28},{4,24},{8,20},{12,16},{16,12},{20,8},{24,4},{28,0},{1,29},{... | collective-permute-start | bytes 1769480 | tf_op jit(solution)/shard_map/ppermute | solution.py:621
  984.8 16.2 %collective-permute-start.54 = (f32[1,144,8,128]{3,2,1,0:T(8,128)}, f32[1,144,8,128]{3,2,1,0:T(8,128)}, u32[]{:S(2)}, u32[]{:S(2)}) collective-permute-start(f32[1,144,8,128]{3,2,1,0:T(8,128)} %get-tuple-element.291), channel_id=1, source_target_pairs={{0,12},{4,8},{8,4},{12,0},{16,28},{20,24},{24,20},{28,16},{1,13},{... | collective-permute-start | bytes 1769480 | tf_op jit(solution)/shard_map/ppermute | solution.py:621
  1017.7 15.5 %collective-permute-done.54.rest_3_ = f32[1,144,8,128]{3,2,1,0:T(8,128)} collective-permute-done((f32[1,144,8,128]{3,2,1,0:T(8,128)}, f32[1,144,8,128]{3,2,1,0:T(8,128)}, u32[]{:S(2)}, u32[]{:S(2)}) %collective-permute-start.54) | collective-permute-done | bytes 589856 | tf_op jit(solution)/shard_map/ppermute | solution.py:621
  (323 shorter events, 238.4 us)
Async XLA Ops:
  190.4 92.9 %collective-permute-start.25 = (f32[4,36,8,128]{3,2,1,0:T(8,128)S(1)}, f32[4,36,8,128]{3,2,1,0:T(8,128)S(1)}, u32[]{:S(2)}, u32[]{:S(2)}) collective-permute-start(f32[4,36,8,128]{3,2,1,0:T(8,128)S(1)} %get-tuple-element.236), channel_id=1, source_target_pairs={{0,16},{4,20},{8,24},{12,28},{16,0},{20,4},{24,8},{28,12},{1,17},{... | collective-permute-start | bytes 1769480 | tf_op jit(solution)/shard_map/ppermute | solution.py:578
  194.0 90.7 %collective-permute-start.29 = (f32[4,36,8,128]{3,2,1,0:T(8,128)S(1)}, f32[4,36,8,128]{3,2,1,0:T(8,128)}, u32[]{:S(2)}, u32[]{:S(2)}) collective-permute-start(f32[4,36,8,128]{3,2,1,0:T(8,128)S(1)} %get-tuple-element.240), channel_id=1, source_target_pairs={{0,20},{4,16},{8,28},{12,24},{16,4},{20,0},{24,12},{28,8},{1,21},{... | collective-permute-start | bytes 1769480 | tf_op jit(solution)/shard_map/ppermute | solution.py:578
  249.2 182.4 %collective-permute-start.12 = (f32[36,4,4096]{2,1,0:T(4,128)S(1)}, f32[36,4,4096]{2,1,0:T(4,128)S(1)}, u32[]{:S(2)}, u32[]{:S(2)}) collective-permute-start(f32[36,4,4096]{2,1,0:T(4,128)S(1)} %get-tuple-element.328), channel_id=1, source_target_pairs={{0,1},{1,2},{2,3},{4,5},{5,6},{6,7},{8,9},{9,10},{10,11},{12,13},{... | collective-permute-start | bytes 7077896 | tf_op jit(solution)/shard_map/ppermute | solution.py:542
  283.3 149.7 %collective-permute-start.11 = (f32[36,4,4096]{2,1,0:T(4,128)S(1)}, f32[36,4,4096]{2,1,0:T(4,128)S(1)}, u32[]{:S(2)}, u32[]{:S(2)}) collective-permute-start(f32[36,4,4096]{2,1,0:T(4,128)S(1)} %get-tuple-element.329), channel_id=1, source_target_pairs={{1,0},{2,1},{3,2},{5,4},{6,5},{7,6},{9,8},{10,9},{11,10},{13,12},{... | collective-permute-start | bytes 7077896 | tf_op jit(solution)/shard_map/ppermute | solution.py:541
  302.1 74.1 %collective-permute-start.26 = (f32[4,36,8,128]{3,2,1,0:T(8,128)S(1)}, f32[4,36,8,128]{3,2,1,0:T(8,128)S(1)}, u32[]{:S(2)}, u32[]{:S(2)}) collective-permute-start(f32[4,36,8,128]{3,2,1,0:T(8,128)S(1)} %get-tuple-element.237), channel_id=1, source_target_pairs={{0,16},{4,20},{8,24},{12,28},{16,0},{20,4},{24,8},{28,12},{1,17},{... | collective-permute-start | bytes 1769480 | tf_op jit(solution)/shard_map/ppermute | solution.py:578
  324.1 78.2 %collective-permute-start.30 = (f32[4,36,8,128]{3,2,1,0:T(8,128)S(1)}, f32[4,36,8,128]{3,2,1,0:T(8,128)S(1)}, u32[]{:S(2)}, u32[]{:S(2)}) collective-permute-start(f32[4,36,8,128]{3,2,1,0:T(8,128)S(1)} %get-tuple-element.241), channel_id=1, source_target_pairs={{0,20},{4,16},{8,28},{12,24},{16,4},{20,0},{24,12},{28,8},{1,21},{... | collective-permute-start | bytes 1769480 | tf_op jit(solution)/shard_map/ppermute | solution.py:578
  325.1 77.9 %collective-permute-start.34 = (f32[4,36,8,128]{3,2,1,0:T(8,128)S(1)}, f32[4,36,8,128]{3,2,1,0:T(8,128)S(1)}, u32[]{:S(2)}, u32[]{:S(2)}) collective-permute-start(f32[4,36,8,128]{3,2,1,0:T(8,128)S(1)} %get-tuple-element.245), channel_id=1, source_target_pairs={{0,24},{4,28},{8,16},{12,20},{16,8},{20,12},{24,0},{28,4},{1,25},{... | collective-permute-start | bytes 1769480 | tf_op jit(solution)/shard_map/ppermute | solution.py:578
  414.7 70.7 %collective-permute-start.23 = (f32[4,36,8,128]{3,2,1,0:T(8,128)S(1)}, f32[4,36,8,128]{3,2,1,0:T(8,128)S(1)}, u32[]{:S(2)}, u32[]{:S(2)}) collective-permute-start(f32[4,36,8,128]{3,2,1,0:T(8,128)S(1)} %get-tuple-element.234), channel_id=1, source_target_pairs={{0,12},{4,8},{8,4},{12,0},{16,28},{20,24},{24,20},{28,16},{1,13},{... | collective-permute-start | bytes 1769480 | tf_op jit(solution)/shard_map/ppermute | solution.py:578
  427.8 67.8 %collective-permute-start.27 = (f32[4,36,8,128]{3,2,1,0:T(8,128)S(1)}, f32[4,36,8,128]{3,2,1,0:T(8,128)S(1)}, u32[]{:S(2)}, u32[]{:S(2)}) collective-permute-start(f32[4,36,8,128]{3,2,1,0:T(8,128)S(1)} %get-tuple-element.238), channel_id=1, source_target_pairs={{0,16},{4,20},{8,24},{12,28},{16,0},{20,4},{24,8},{28,12},{1,17},{... | collective-permute-start | bytes 1769480 | tf_op jit(solution)/shard_map/ppermute | solution.py:578
  427.8 81.1 %collective-permute-start.31 = (f32[4,36,8,128]{3,2,1,0:T(8,128)S(1)}, f32[4,36,8,128]{3,2,1,0:T(8,128)S(1)}, u32[]{:S(2)}, u32[]{:S(2)}) collective-permute-start(f32[4,36,8,128]{3,2,1,0:T(8,128)S(1)} %get-tuple-element.242), channel_id=1, source_target_pairs={{0,20},{4,16},{8,28},{12,24},{16,4},{20,0},{24,12},{28,8},{1,21},{... | collective-permute-start | bytes 1769480 | tf_op jit(solution)/shard_map/ppermute | solution.py:578
  431.6 77.4 %collective-permute-start.35 = (f32[4,36,8,128]{3,2,1,0:T(8,128)S(1)}, f32[4,36,8,128]{3,2,1,0:T(8,128)S(1)}, u32[]{:S(2)}, u32[]{:S(2)}) collective-permute-start(f32[4,36,8,128]{3,2,1,0:T(8,128)S(1)} %get-tuple-element.246), channel_id=1, source_target_pairs={{0,24},{4,28},{8,16},{12,20},{16,8},{20,12},{24,0},{28,4},{1,25},{... | collective-permute-start | bytes 1769480 | tf_op jit(solution)/shard_map/ppermute | solution.py:578
  434.5 87.1 %collective-permute-start.39 = (f32[4,36,8,128]{3,2,1,0:T(8,128)S(1)}, f32[4,36,8,128]{3,2,1,0:T(8,128)S(1)}, u32[]{:S(2)}, u32[]{:S(2)}) collective-permute-start(f32[4,36,8,128]{3,2,1,0:T(8,128)S(1)} %get-tuple-element.250), channel_id=1, source_target_pairs={{0,28},{4,24},{8,20},{12,16},{16,12},{20,8},{24,4},{28,0},{1,29},{... | collective-permute-start | bytes 1769480 | tf_op jit(solution)/shard_map/ppermute | solution.py:578
  559.2 63.0 %collective-permute-start.43 = (f32[3,36,8,128]{3,2,1,0:T(8,128)S(1)}, f32[3,36,8,128]{3,2,1,0:T(8,128)S(1)}, u32[]{:S(2)}, u32[]{:S(2)}) collective-permute-start(f32[3,36,8,128]{3,2,1,0:T(8,128)S(1)} %get-tuple-element.267), channel_id=1, source_target_pairs={{0,12},{4,8},{8,4},{12,0},{16,28},{20,24},{24,20},{28,16},{1,13},{... | collective-permute-start | bytes 1327112 | tf_op jit(solution)/shard_map/ppermute | solution.py:578
  560.1 63.1 %collective-permute-start.44 = (f32[3,36,8,128]{3,2,1,0:T(8,128)S(1)}, f32[3,36,8,128]{3,2,1,0:T(8,128)S(1)}, u32[]{:S(2)}, u32[]{:S(2)}) collective-permute-start(f32[3,36,8,128]{3,2,1,0:T(8,128)S(1)} %get-tuple-element.271), channel_id=1, source_target_pairs={{0,16},{4,20},{8,24},{12,28},{16,0},{20,4},{24,8},{28,12},{1,17},{... | collective-permute-start | bytes 1327112 | tf_op jit(solution)/shard_map/ppermute | solution.py:578
  625.8 81.1 %collective-permute-start.72 = (f32[1,144,8,128]{3,2,1,0:T(8,128)}, f32[1,144,8,128]{3,2,1,0:T(8,128)}, u32[]{:S(2)}, u32[]{:S(2)}) collective-permute-start(f32[1,144,8,128]{3,2,1,0:T(8,128)} %get-tuple-element.320), channel_id=1, source_target_pairs={{0,16},{4,20},{8,24},{12,28},{16,0},{20,4},{24,8},{28,12},{1,17},{... | collective-permute-start | bytes 1769480 | tf_op jit(solution)/shard_map/ppermute | solution.py:621
  632.3 87.2 %collective-permute-start.73 = (f32[1,144,8,128]{3,2,1,0:T(8,128)}, f32[1,144,8,128]{3,2,1,0:T(8,128)}, u32[]{:S(2)}, u32[]{:S(2)}) collective-permute-start(f32[1,144,8,128]{3,2,1,0:T(8,128)} %get-tuple-element.321), channel_id=1, source_target_pairs={{0,20},{4,16},{8,28},{12,24},{16,4},{20,0},{24,12},{28,8},{1,21},{... | collective-permute-start | bytes 1769480 | tf_op jit(solution)/shard_map/ppermute | solution.py:621
  681.7 77.9 %collective-permute-start.62 = (f32[1,144,8,128]{3,2,1,0:T(8,128)}, f32[1,144,8,128]{3,2,1,0:T(8,128)S(1)}, u32[]{:S(2)}, u32[]{:S(2)}) collective-permute-start(f32[1,144,8,128]{3,2,1,0:T(8,128)} %get-tuple-element.301), channel_id=1, source_target_pairs={{0,4},{4,0},{8,12},{12,8},{16,20},{20,16},{24,28},{28,24},{1,5},{5... | collective-permute-start | bytes 1769480 | tf_op jit(solution)/shard_map/ppermute | solution.py:621
  706.9 87.0 %collective-permute-start.63 = (f32[1,144,8,128]{3,2,1,0:T(8,128)}, f32[1,144,8,128]{3,2,1,0:T(8,128)}, u32[]{:S(2)}, u32[]{:S(2)}) collective-permute-start(f32[1,144,8,128]{3,2,1,0:T(8,128)} %get-tuple-element.302), channel_id=1, source_target_pairs={{0,8},{4,12},{8,0},{12,4},{16,24},{20,28},{24,16},{28,20},{1,9},{5... | collective-permute-start | bytes 1769480 | tf_op jit(solution)/shard_map/ppermute | solution.py:621
  719.6 76.8 %collective-permute-start.64 = (f32[1,144,8,128]{3,2,1,0:T(8,128)}, f32[1,144,8,128]{3,2,1,0:T(8,128)}, u32[]{:S(2)}, u32[]{:S(2)}) collective-permute-start(f32[1,144,8,128]{3,2,1,0:T(8,128)} %get-tuple-element.303), channel_id=1, source_target_pairs={{0,12},{4,8},{8,4},{12,0},{16,28},{20,24},{24,20},{28,16},{1,13},{... | collective-permute-start | bytes 1769480 | tf_op jit(solution)/shard_map/ppermute | solution.py:621
  719.6 84.2 %collective-permute-start.65 = (f32[1,144,8,128]{3,2,1,0:T(8,128)}, f32[1,144,8,128]{3,2,1,0:T(8,128)}, u32[]{:S(2)}, u32[]{:S(2)}) collective-permute-start(f32[1,144,8,128]{3,2,1,0:T(8,128)} %get-tuple-element.304), channel_id=1, source_target_pairs={{0,16},{4,20},{8,24},{12,28},{16,0},{20,4},{24,8},{28,12},{1,17},{... | collective-permute-start | bytes 1769480 | tf_op jit(solution)/shard_map/ppermute | solution.py:621
  739.8 81.0 %collective-permute-start.66 = (f32[1,144,8,128]{3,2,1,0:T(8,128)}, f32[1,144,8,128]{3,2,1,0:T(8,128)}, u32[]{:S(2)}, u32[]{:S(2)}) collective-permute-start(f32[1,144,8,128]{3,2,1,0:T(8,128)} %get-tuple-element.305), channel_id=1, source_target_pairs={{0,20},{4,16},{8,28},{12,24},{16,4},{20,0},{24,12},{28,8},{1,21},{... | collective-permute-start | bytes 1769480 | tf_op jit(solution)/shard_map/ppermute | solution.py:621
  793.9 78.1 %collective-permute-start.68 = (f32[1,144,8,128]{3,2,1,0:T(8,128)S(1)}, f32[1,144,8,128]{3,2,1,0:T(8,128)S(1)}, u32[]{:S(2)}, u32[]{:S(2)}) collective-permute-start(f32[1,144,8,128]{3,2,1,0:T(8,128)S(1)} %copy-done.72), channel_id=1, source_target_pairs={{0,28},{4,24},{8,20},{12,16},{16,12},{20,8},{24,4},{28,0},{1,29},{... | collective-permute-start | bytes 1769480 | tf_op jit(solution)/shard_map/ppermute | solution.py:621
  796.4 75.8 %collective-permute-start.55 = (f32[1,144,8,128]{3,2,1,0:T(8,128)}, f32[1,144,8,128]{3,2,1,0:T(8,128)S(1)}, u32[]{:S(2)}, u32[]{:S(2)}) collective-permute-start(f32[1,144,8,128]{3,2,1,0:T(8,128)} %get-tuple-element.293), channel_id=1, source_target_pairs={{0,4},{4,0},{8,12},{12,8},{16,20},{20,16},{24,28},{28,24},{1,5},{5... | collective-permute-start | bytes 1769480 | tf_op jit(solution)/shard_map/ppermute | solution.py:621
  803.8 70.0 %collective-permute-start.56 = (f32[1,144,8,128]{3,2,1,0:T(8,128)}, f32[1,144,8,128]{3,2,1,0:T(8,128)S(1)}, u32[]{:S(2)}, u32[]{:S(2)}) collective-permute-start(f32[1,144,8,128]{3,2,1,0:T(8,128)} %get-tuple-element.294), channel_id=1, source_target_pairs={{0,8},{4,12},{8,0},{12,4},{16,24},{20,28},{24,16},{28,20},{1,9},{5... | collective-permute-start | bytes 1769480 | tf_op jit(solution)/shard_map/ppermute | solution.py:621
  820.8 88.4 %collective-permute-start.58 = (f32[1,144,8,128]{3,2,1,0:T(8,128)}, f32[1,144,8,128]{3,2,1,0:T(8,128)}, u32[]{:S(2)}, u32[]{:S(2)}) collective-permute-start(f32[1,144,8,128]{3,2,1,0:T(8,128)} %get-tuple-element.296), channel_id=1, source_target_pairs={{0,16},{4,20},{8,24},{12,28},{16,0},{20,4},{24,8},{28,12},{1,17},{... | collective-permute-start | bytes 1769480 | tf_op jit(solution)/shard_map/ppermute | solution.py:621
  873.7 74.8 %collective-permute-start.61 = (f32[1,144,8,128]{3,2,1,0:T(8,128)}, f32[1,144,8,128]{3,2,1,0:T(8,128)}, u32[]{:S(2)}, u32[]{:S(2)}) collective-permute-start(f32[1,144,8,128]{3,2,1,0:T(8,128)} %get-tuple-element.299), channel_id=1, source_target_pairs={{0,28},{4,24},{8,20},{12,16},{16,12},{20,8},{24,4},{28,0},{1,29},{... | collective-permute-start | bytes 1769480 | tf_op jit(solution)/shard_map/ppermute | solution.py:621
  876.9 73.2 %collective-permute-start.52 = (f32[1,144,8,128]{3,2,1,0:T(8,128)}, f32[1,144,8,128]{3,2,1,0:T(8,128)}, u32[]{:S(2)}, u32[]{:S(2)}) collective-permute-start(f32[1,144,8,128]{3,2,1,0:T(8,128)} %get-tuple-element.289), channel_id=1, source_target_pairs={{0,4},{4,0},{8,12},{12,8},{16,20},{20,16},{24,28},{28,24},{1,5},{5... | collective-permute-start | bytes 1769480 | tf_op jit(solution)/shard_map/ppermute | solution.py:621
  909.2 75.7 %collective-permute-start.53 = (f32[1,144,8,128]{3,2,1,0:T(8,128)}, f32[1,144,8,128]{3,2,1,0:T(8,128)}, u32[]{:S(2)}, u32[]{:S(2)}) collective-permute-start(f32[1,144,8,128]{3,2,1,0:T(8,128)} %get-tuple-element.290), channel_id=1, source_target_pairs={{0,8},{4,12},{8,0},{12,4},{16,24},{20,28},{24,16},{28,20},{1,9},{5... | collective-permute-start | bytes 1769480 | tf_op jit(solution)/shard_map/ppermute | solution.py:621
  928.2 108.2 %collective-permute-start.48 = (f32[1,144,8,128]{3,2,1,0:T(8,128)}, f32[1,144,8,128]{3,2,1,0:T(8,128)S(1)}, u32[]{:S(2)}, u32[]{:S(2)}) collective-permute-start(f32[1,144,8,128]{3,2,1,0:T(8,128)} %get-tuple-element.284), channel_id=1, source_target_pairs={{0,16},{4,20},{8,24},{12,28},{16,0},{20,4},{24,8},{28,12},{1,17},{... | collective-permute-start | bytes 1769480 | tf_op jit(solution)/shard_map/ppermute | solution.py:621
  928.2 108.2 %collective-permute-start.49 = (f32[1,144,8,128]{3,2,1,0:T(8,128)}, f32[1,144,8,128]{3,2,1,0:T(8,128)}, u32[]{:S(2)}, u32[]{:S(2)}) collective-permute-start(f32[1,144,8,128]{3,2,1,0:T(8,128)} %get-tuple-element.285), channel_id=1, source_target_pairs={{0,20},{4,16},{8,28},{12,24},{16,4},{20,0},{24,12},{28,8},{1,21},{... | collective-permute-start | bytes 1769480 | tf_op jit(solution)/shard_map/ppermute | solution.py:621
  948.6 87.9 %collective-permute-start.50 = (f32[1,144,8,128]{3,2,1,0:T(8,128)}, f32[1,144,8,128]{3,2,1,0:T(8,128)}, u32[]{:S(2)}, u32[]{:S(2)}) collective-permute-start(f32[1,144,8,128]{3,2,1,0:T(8,128)} %get-tuple-element.286), channel_id=1, source_target_pairs={{0,24},{4,28},{8,16},{12,20},{16,8},{20,12},{24,0},{28,4},{1,25},{... | collective-permute-start | bytes 1769480 | tf_op jit(solution)/shard_map/ppermute | solution.py:621
  950.1 86.3 %collective-permute-start.51 = (f32[1,144,8,128]{3,2,1,0:T(8,128)}, f32[1,144,8,128]{3,2,1,0:T(8,128)}, u32[]{:S(2)}, u32[]{:S(2)}) collective-permute-start(f32[1,144,8,128]{3,2,1,0:T(8,128)} %get-tuple-element.287), channel_id=1, source_target_pairs={{0,28},{4,24},{8,20},{12,16},{16,12},{20,8},{24,4},{28,0},{1,29},{... | collective-permute-start | bytes 1769480 | tf_op jit(solution)/shard_map/ppermute | solution.py:621
  (117 other events, 5937.5 us)
